TPU v7x, 16 devices: a 4x2x1 block of a 4x4x8 slice. The times are simulated.
16 devices in a mesh: dp: 2 (over y, z), tp: 8 (over x, core).
Axes of the slice: x: 4, y: 2, z: 1, core: 2. Of those that a mesh axis runs over, the one named last changes fastest.
The devices are a block of a 4x4x8 slice.
Arguments:
- tok_hidden: bfloat16 [256, 2048], P('dp'), parts along dimension 0
- seq_lens: int32 [256], P('dp'), parts along dimension 0
- k_cache: bfloat16 [256, 512, 8, 64], P('dp', None, 'tp'), parts along dimension 0
- v_cache: bfloat16 [256, 512, 8, 64], P('dp', None, 'tp'), parts along dimension 0
- next_tok: int32 [256], P('dp'), parts along dimension 0
- g_attn: bfloat16 [2048], replicated
- w_q: bfloat16 [2048, 2048], P(None, 'tp')
- b_q: bfloat16 [2048], P('tp')
- w_k: bfloat16 [2048, 512], P(None, 'tp')
- b_k: bfloat16 [512], P('tp')
- w_v: bfloat16 [2048, 512], P(None, 'tp')
- b_v: bfloat16 [512], P('tp')
- w_o: bfloat16 [2048, 2048], P('tp')
- g_mlp: bfloat16 [2048], replicated
- w_gate: bfloat16 [2048, 8192], P(None, 'tp')
- w_up: bfloat16 [2048, 8192], P(None, 'tp')
- w_down: bfloat16 [8192, 2048], P('tp')
- g_final: bfloat16 [2048], replicated
- w_head: bfloat16 [128256, 2048], P('tp')
Outputs:
- output 1: bfloat16 [256, 2048], P('dp'), parts along dimension 0
- output 2: bfloat16 [256, 512, 8, 64], P('dp', None, 'tp'), parts along dimension 0
- output 3: bfloat16 [256, 512, 8, 64], P('dp', None, 'tp'), parts along dimension 0
- output 4: float32 [256], P('dp'), parts along dimension 0
- output 5: float32 [256], P('dp'), parts along dimension 0
There are 2 independent parts. A program takes and returns all parts, laid end to end along the dimension named above; an argument that names none is the same for every part.
All inputs are finite; a program needn't handle non-finite values.
Results may differ from a plain program's by a relative error of at most 0.0139837.
Values are sent between devices in bfloat16 or wider.
A program may use at most 768 MiB of HBM per device.

v0:
```python
import jax
import jax.numpy as jnp
from jax import lax
from jax.sharding import PartitionSpec as P

THETA = 1000000.0
EPS = 1e-6


def rms_norm(values, gain_vec):
    vals_f32 = values.astype(jnp.float32)
    inv_rms = lax.rsqrt(jnp.mean(vals_f32 * vals_f32, axis=-1, keepdims=True) + EPS)
    return (vals_f32 * inv_rms * gain_vec.astype(jnp.float32)).astype(jnp.bfloat16)


def rotary(values, positions):
    half_dim = values.shape[-1] // 2
    inv_freq = jnp.power(THETA, jnp.arange(half_dim, dtype=jnp.float32) * (-2.0 / values.shape[-1]))
    angles = positions.astype(jnp.float32)[:, None] * inv_freq[None, :]
    cos_part = jnp.cos(angles)[:, None, :]
    sin_part = jnp.sin(angles)[:, None, :]
    first_half = values[..., :half_dim]
    second_half = values[..., half_dim:]
    return jnp.concatenate([first_half * cos_part - second_half * sin_part, second_half * cos_part + first_half * sin_part], axis=-1)


def attention_block(tok_hidden, seq_lens, k_cache, v_cache, g_attn, w_q, b_q, w_k, b_k, w_v, b_v):
    num_rows = tok_hidden.shape[0]
    cache_len = k_cache.shape[1]
    slot_count = k_cache.shape[2]
    head_dim = k_cache.shape[3]
    head_count = w_q.shape[1] // head_dim
    group_size = head_count // slot_count
    normed = rms_norm(tok_hidden, g_attn)
    q_proj = jnp.dot(normed, w_q, preferred_element_type=jnp.float32) + b_q.astype(jnp.float32)
    k_proj = jnp.dot(normed, w_k, preferred_element_type=jnp.float32) + b_k.astype(jnp.float32)
    v_proj = jnp.dot(normed, w_v, preferred_element_type=jnp.float32) + b_v.astype(jnp.float32)
    q_rot = rotary(q_proj.reshape(num_rows, head_count, head_dim), seq_lens).astype(jnp.bfloat16)
    k_new = rotary(k_proj.reshape(num_rows, slot_count, head_dim), seq_lens).astype(jnp.bfloat16)
    v_new = v_proj.reshape(num_rows, slot_count, head_dim).astype(jnp.bfloat16)
    slot_ids = lax.broadcasted_iota(jnp.int32, (1, cache_len, 1, 1), 1)
    write_mask = slot_ids == seq_lens[:, None, None, None]
    k_all = jnp.where(write_mask, k_new[:, None], k_cache)
    v_all = jnp.where(write_mask, v_new[:, None], v_cache)
    q_grp = q_rot.reshape(num_rows, slot_count, group_size, head_dim)
    scores = jnp.einsum('bkgd,blkd->bkgl', q_grp, k_all, preferred_element_type=jnp.float32) * (head_dim ** -0.5)
    score_ids = lax.broadcasted_iota(jnp.int32, (1, 1, 1, cache_len), 3)
    scores = jnp.where(score_ids <= seq_lens[:, None, None, None], scores, -jnp.inf)
    row_max = jnp.max(scores, axis=-1, keepdims=True)
    exp_scores = jnp.exp(scores - row_max)
    attn_probs = (exp_scores / jnp.sum(exp_scores, axis=-1, keepdims=True)).astype(jnp.bfloat16)
    attn_vals = jnp.einsum('bkgl,blkd->bkgd', attn_probs, v_all, preferred_element_type=jnp.float32)
    attn_out = attn_vals.astype(jnp.bfloat16).reshape(num_rows, head_count * head_dim)
    return attn_out, k_all, v_all


def local_step(tok_hidden, seq_lens, k_cache, v_cache, next_tok, g_attn, w_q, b_q, w_k, b_k, w_v, b_v, w_o, g_mlp, w_gate, w_up, w_down, g_final, w_head):
    attn_out, k_all, v_all = attention_block(tok_hidden, seq_lens, k_cache, v_cache, g_attn, w_q, b_q, w_k, b_k, w_v, b_v)
    attn_part = jnp.dot(attn_out, w_o, preferred_element_type=jnp.float32).astype(jnp.bfloat16)
    attn_sum = lax.psum(attn_part, 'tp')
    residual = (tok_hidden.astype(jnp.float32) + attn_sum.astype(jnp.float32)).astype(jnp.bfloat16)
    mlp_in = rms_norm(residual, g_mlp)
    gate_proj = jnp.dot(mlp_in, w_gate, preferred_element_type=jnp.float32)
    up_proj = jnp.dot(mlp_in, w_up, preferred_element_type=jnp.float32)
    hidden = (jax.nn.silu(gate_proj) * up_proj).astype(jnp.bfloat16)
    down_part = jnp.dot(hidden, w_down, preferred_element_type=jnp.float32).astype(jnp.bfloat16)
    down_sum = lax.psum(down_part, 'tp')
    y_out = (residual.astype(jnp.float32) + down_sum.astype(jnp.float32)).astype(jnp.bfloat16)
    final_norm = rms_norm(y_out, g_final)
    logits = lax.dot_general(final_norm, w_head, (((1,), (1,)), ((), ())), preferred_element_type=jnp.float32)
    vocab_loc = w_head.shape[0]
    vocab_ids = lax.broadcasted_iota(jnp.int32, (1, vocab_loc), 1)
    local_tok = next_tok - lax.axis_index('tp') * vocab_loc
    local_max = jnp.max(logits, axis=1)
    local_sum = jnp.sum(jnp.exp(logits - local_max[:, None]), axis=1)
    local_target = jnp.sum(jnp.where(vocab_ids == local_tok[:, None], logits, 0.0), axis=1)
    all_stats = lax.all_gather(jnp.stack([local_max, local_sum, local_target]), 'tp')
    glob_max = jnp.max(all_stats[:, 0], axis=0)
    exp_total = jnp.sum(all_stats[:, 1] * jnp.exp(all_stats[:, 0] - glob_max[None, :]), axis=0)
    norm_lse = glob_max + jnp.log(exp_total)
    tok_logp = jnp.sum(all_stats[:, 2], axis=0) - norm_lse
    return y_out, k_all, v_all, tok_logp, norm_lse


def solution(mesh):
    row_spec = P('dp', None)
    vec_spec = P('dp')
    cache_spec = P('dp', None, 'tp', None)
    col_spec = P(None, 'tp')
    part_spec = P('tp')
    whole_spec = P(None)
    in_specs = (row_spec, vec_spec, cache_spec, cache_spec, vec_spec, whole_spec, col_spec, part_spec, col_spec, part_spec, col_spec, part_spec, P('tp', None), whole_spec, col_spec, col_spec, P('tp', None), whole_spec, P('tp', None))
    out_specs = (row_spec, cache_spec, cache_spec, vec_spec, vec_spec)
    return jax.shard_map(local_step, mesh=mesh, in_specs=in_specs, out_specs=out_specs, check_vma=False)
```

profile of v0, /device:TPU:112, one launch (start us, length us, event | category | flops | bytes accessed | tf_op | source)
XLA Modules:
  0.0 218.8 jit_solution(15261698451144249936)
XLA Ops:
  7.2 0.0 copy-start
  7.2 0.1 all-reduce.3.cloned.1.call-start
  7.3 0.7 convert_element_type.89
  8.0 0.8 iota_compare_fusion.2
  8.8 0.7 convert_element_type.86
  9.5 1.2 fusion.22
  10.7 0.7 convert_element_type.90
  11.4 0.3 multiply_cosine_fusion
  11.7 1.5 fusion.17
  13.2 0.1 fusion.57
  13.4 0.1 copy.37
  13.5 0.7 convert_element_type.92
  14.1 1.5 fusion.18
  15.6 0.1 copy.38
  15.7 0.7 convert_element_type.88
  16.4 1.7 convolution_add_fusion
  18.2 0.1 copy.34
  18.3 0.1 copy.41
  18.4 0.1 copy.42
  18.6 0.1 subtract_convert_fusion
  18.7 12.0 %broadcast_select_fusion.1 = (bf16[128,512,1,64]{1,3,2,0:T(8,128)(2,1)}, bf16[128,512,1,64]{1,3,2,0:T(8,128)(2,1)}) fusion(bf16[128,512,1,64]{1,3,2,0:T(8,128)(2,1)} %param.21, pred[128,512]{1,0:T(8,128)(4,1)S(1)} %get-tuple-element.28, bf16[128,64]{1,0:T(8,128)(2,1)S(1)} %copy.37, bf16[128,512,1,64]{1,3,2,0:T(8,128)(2,1)} %param.22, bf16[128,64]{1,0:T(8,128)(2,1)S(1)} %copy.38), kind=kLoop, calls=%fused_computation.6 | loop fusion | flops 8388608 | bytes 33652736 | tf_op jit(solution)/shard_map/jit(_where)/select_n | solution.py:43
  30.8 5.0 %fusion.67 = (f32[128,4]{1,0:T(8,128)S(1)}, f32[128,4,512]{2,1,0:T(4,128)S(1)}) fusion(bf16[128,512,1,64]{1,3,2,0:T(8,128)(2,1)} %get-tuple-element.19, pred[128,512]{1,0:T(8,128)(4,1)S(1)} %get-tuple-element.27, bf16[128,4,32]{2,1,0:T(4,128)(2,1)S(1)} %get-tuple-element.16, bf16[128,4,32]{2,1,0:T(4,128)(2,1)S(1)} %get-tuple-element.15), kind=kOutput, calls=%fused_computation.91 | convolution fusion | flops 34734592 | bytes 9570304 | tf_op jit(solution)/shard_map/sub | solution.py:50
  35.8 0.0 copy-start.4
  35.8 0.0 copy-start.3
  35.8 5.8 %fusion.11 = bf16[128,4,64]{2,1,0:T(4,128)(2,1)S(1)} fusion(bf16[128,512,1,64]{1,3,2,0:T(8,128)(2,1)} %get-tuple-element.20, f32[128,4,512]{2,1,0:T(4,128)S(1)} %get-tuple-element.30, f32[128,4]{1,0:T(8,128)S(1)} %get-tuple-element.29), kind=kOutput, calls=%fused_computation.25 | convolution fusion | flops 34111488 | bytes 9504768 | tf_op jit(solution)/shard_map/bkgl,blkd->bkgd/dot_general | solution.py:52
  41.5 0.1 copy.39
  41.7 0.0 copy-done
  41.7 1.1 convolution_convert_fusion.1
  42.8 0.1 all-reduce.3.cloned.1.call-update
  42.9 0.2 all-reduce.5.cloned.1.call-start
  43.1 0.0 copy-done.4
  43.1 55.5 %all-reduce.3.cloned.1.call-done = bf16[128,2048]{1,0:T(8,128)(2,1)} async-done(((bf16[128,2048]{1,0:T(8,128)(2,1)}), bf16[128,2048]{1,0:T(8,128)(2,1)}) %all-reduce.3.cloned.1.call-update) | async-done | bytes 524304 | tf_op jit(solution)/shard_map/psum | solution.py:60
  98.7 0.0 copy-done.3
  98.7 1.3 fusion.26
  100.0 0.0 copy-start.5
  100.0 0.0 copy-start.6
  100.0 3.0 %fusion.43 = f32[128,1024]{1,0:T(8,128)S(1)} fusion(bf16[2048,1024]{1,0:T(8,128)(2,1)} %param.33, bf16[128,2048]{1,0:T(8,128)(2,1)S(1)} %get-tuple-element.14, f32[2048]{0:T(1024)S(1)} %convert_element_type.99, f32[128]{0:T(128)S(1)} %add_rsqrt_fusion.1), kind=kOutput, calls=%fused_computation.58 | convolution fusion | flops 537919488 | bytes 5251584 | tf_op jit(solution)/shard_map/dot_general | solution.py:63
  103.0 5.7 %convolution_convert_fusion = bf16[128,2048]{1,0:T(8,128)(2,1)} fusion(bf16[1024,2048]{1,0:T(8,128)(2,1)} %param.35, bf16[2048,1024]{1,0:T(8,128)(2,1)} %param.34, f32[128,1024]{1,0:T(8,128)S(1)} %fusion.43, bf16[128,2048]{1,0:T(8,128)(2,1)S(1)} %get-tuple-element.14, f32[2048]{0:T(1024)S(1)} %convert_element_type.99, f32[128]{0:T(128)S(1)} %add_rsqrt_fusion.1), kind=kOutput, calls=%fused_computation.10 | convolution fusion | flops 1075838976 | bytes 9970176 | tf_op jit(solution)/shard_map/dot_general | solution.py:66
  108.7 0.1 all-reduce.5.cloned.1.call-update
  108.7 0.0 copy-done.5
  108.8 0.0 copy-done.6
  108.8 52.0 %all-reduce.5.cloned.1.call-done = bf16[128,2048]{1,0:T(8,128)(2,1)} async-done(((bf16[128,2048]{1,0:T(8,128)(2,1)}), bf16[128,2048]{1,0:T(8,128)(2,1)}) %all-reduce.5.cloned.1.call-update) | async-done | bytes 524304 | tf_op jit(solution)/shard_map/psum | solution.py:67
  160.8 1.3 fusion.19
  162.1 0.0 copy-start.2
  162.1 0.0 copy-start.1
  162.1 26.2 %fusion.68 = (f32[128]{0:T(128)S(1)}, f32[128,16032]{0,1:T(8,128)S(1)}) fusion(bf16[16032,2048]{1,0:T(8,128)(2,1)} %param.37, bf16[128,2048]{1,0:T(8,128)(2,1)S(1)} %get-tuple-element.12, f32[2048]{0:T(1024)S(1)} %convert_element_type.106, f32[128]{0:T(128)S(1)} %add_rsqrt_fusion), kind=kOutput, calls=%fused_computation.92 | convolution fusion | flops 8408485888 | bytes 74408960 | tf_op jit(solution)/shard_map/dot_general | solution.py:70
  188.4 0.0 copy-done.2
  188.4 2.2 exponential_reduce_fusion
  190.6 20.8 %all-gather.1 = f32[8,3,128]{2,1,0:T(4,128)S(1)} all-gather(f32[1,3,128]{2,1,0:T(4,128)S(1)} %maximum_bitcast_fusion), channel_id=2, replica_groups=mesh['dp'=2,'tp'=8] {'tp'}, dimensions={0}, use_global_device_ids=true | all-gather | bytes 13824 | tf_op jit(solution)/shard_map/all_gather | solution.py:77
  211.4 0.5 fusion.63
  212.0 0.0 copy-done.1
  (12 shorter events, 0.1 us)
Async XLA Ops:
  7.2 34.5 %copy-start = (bf16[256,2048]{1,0:T(8,128)(2,1)S(1)}, bf16[256,2048]{1,0:T(8,128)(2,1)}, u32[]{:S(2)}) copy-start(bf16[256,2048]{1,0:T(8,128)(2,1)} %param.31) | copy-start | bytes 3145732
  7.2 91.5 %all-reduce.3.cloned.1.call-start = ((), (), s32[]{:S(2)}) async-start(), calls=%async_computation | async-start | bytes 1048576 | tf_op jit(solution)/shard_map/psum | solution.py:60
  35.8 7.4 %copy-start.4 = (bf16[2048]{0:T(1024)(128)(2,1)S(1)}, bf16[2048]{0:T(1024)(128)(2,1)}, u32[]{:S(2)}) copy-start(bf16[2048]{0:T(1024)(128)(2,1)} %param.32) | copy-start | bytes 12292
  35.8 62.9 %copy-start.3 = (bf16[128,2048]{1,0:T(8,128)(2,1)S(1)}, bf16[128,2048]{1,0:T(8,128)(2,1)}, u32[]{:S(2)}) copy-start(bf16[128,2048]{1,0:T(8,128)(2,1)} %param.19) | copy-start | bytes 1572868
  42.9 117.9 %all-reduce.5.cloned.1.call-start = ((), (), s32[]{:S(2)}) async-start(), calls=%async_computation.1 | async-start | bytes 1048576 | tf_op jit(solution)/shard_map/psum | solution.py:67
  100.0 8.7 %copy-start.5 = (bf16[2048]{0:T(1024)(128)(2,1)S(1)}, bf16[2048]{0:T(1024)(128)(2,1)}, u32[]{:S(2)}) copy-start(bf16[2048]{0:T(1024)(128)(2,1)} %param.36) | copy-start | bytes 12292
  100.0 8.8 %copy-start.6 = (s32[128]{0:T(128)S(1)}, s32[128]{0:T(128)}, u32[]{:S(2)}) copy-start(s32[128]{0:T(128)} %param.23) | copy-start | bytes 1540
  162.1 26.3 %copy-start.2 = (bf16[128,2048]{1,0:T(8,128)(2,1)}, bf16[128,2048]{1,0:T(8,128)(2,1)S(1)}, u32[]{:S(2)}) copy-start(bf16[128,2048]{1,0:T(8,128)(2,1)S(1)} %get-tuple-element.12) | copy-start | bytes 1572868
  162.1 49.9 %copy-start.1 = (bf16[256,2048]{1,0:T(8,128)(2,1)S(1)}, bf16[256,2048]{1,0:T(8,128)(2,1)}, u32[]{:S(2)}) copy-start(bf16[256,2048]{1,0:T(8,128)(2,1)} %param.31) | copy-start | bytes 3145732
Sparse Core Ops, SparseCore 0:
  43.0 55.6 all-reduce.2
  108.9 51.8 all-reduce.4
where the time goes:
time: 219 us
  waiting for transfers between devices  108 us (49%)
  matrix products  51.5 us (24%)
  other arithmetic  23.5 us (11%)
  blocking collectives  20.8 us (9%)
  between operations  14.3 us (7%)
    psum x1, waiting for transfers between devices, local_step(): attn_sum = lax.psum(attn_part, 'tp')  55.5 us
    psum x1, waiting for transfers between devices, local_step(): down_sum = lax.psum(down_part, 'tp')  52 us
    dot_general x1, matrix products, local_step(): lax.dot_general(final_norm, w_head, (((1,), (1,)), ((), ())), preferred_e...  26.2 us
    all_gather x1, blocking collectives, local_step(): lax.all_gather(jnp.stack([local_max, local_sum, local_target]), 'tp')  20.8 us
    select_n x1, other arithmetic, attention_block(): k_all = jnp.where(write_mask, k_new[:, None], k_cache)  12 us
    dot_general x1, matrix products, attention_block(): jnp.einsum('bkgl,blkd->bkgd', attn_probs, v_all, preferred_element_type=j...  5.77 us
    dot_general x1, matrix products, local_step(): jnp.dot(hidden, w_down, preferred_element_type=jnp.float32)  5.69 us
    sub x1, matrix products, attention_block(): exp_scores = jnp.exp(scores - row_max)  5.01 us
  transfers between devices with their start and end apart: 2, of which 2 were waited for; matrix products, arithmetic and copies ran while one was open for 0% of the time, Pallas kernels for 0%

commit v1 on v0

v1 whole, which is shorter than its diff:
```python
import functools
import numpy as np
import jax
import jax.numpy as jnp
from jax import lax
from jax.experimental import pallas as pl
from jax.experimental.pallas import tpu as pltpu
from jax.sharding import PartitionSpec as P

THETA = 1000000.0
EPS = 1e-6
MESH = pl.DeviceIdType.MESH
NT = (((1,), (1,)), ((), ()))
F32 = jnp.float32
BF16 = jnp.bfloat16


def rms(vals_f32, gain_f32):
    inv_rms = lax.rsqrt(jnp.mean(vals_f32 * vals_f32, axis=-1, keepdims=True) + EPS)
    return (vals_f32 * inv_rms * gain_f32).astype(BF16)


SEQ = 8
SUB = 2


def attn_kernel(lens_s, lens_v, x_ref, g_ref, bq_ref, bk_ref, bv_ref, freq_ref, kc, vc, wq, wk, wv, wo,
                ko, vo, part, kbuf, vbuf, wq_v, wkv_v, wo_v, lens_b, qq, kvt, o_s,
                k_in, v_in, k_out, v_out, w_sem):
    rows = x_ref.shape[0]
    dim = wk.shape[0]
    slots = kbuf.shape[1]
    span = SEQ * SUB * dim
    steps = kbuf.shape[0] // span

    w_copies = [pltpu.make_async_copy(wq, wq_v, w_sem.at[0]),
                pltpu.make_async_copy(wk, wkv_v.at[pl.ds(0, dim)], w_sem.at[1]),
                pltpu.make_async_copy(wv, wkv_v.at[pl.ds(dim, dim)], w_sem.at[2])]
    wo_copy = pltpu.make_async_copy(wo, wo_v, w_sem.at[3])
    for copy in w_copies:
        copy.start()

    def moves(step):
        here = pl.ds(pl.multiple_of(step * span, span), span)
        return (pltpu.make_async_copy(kc.at[here], kbuf.at[here], k_in.at[step]),
                pltpu.make_async_copy(vc.at[here], vbuf.at[here], v_in.at[step]),
                pltpu.make_async_copy(kbuf.at[here], ko.at[here], k_out.at[step]),
                pltpu.make_async_copy(vbuf.at[here], vo.at[here], v_out.at[step]))

    def begin(step, carry):
        k_copy, v_copy, _, _ = moves(step)
        k_copy.start()
        v_copy.start()
        return carry

    lax.fori_loop(0, steps, begin, 0)
    wo_copy.start()

    normed = rms(x_ref[...].astype(F32), g_ref[...].astype(F32).reshape(1, -1))
    lens_row = lens_v[...].reshape(1, rows).astype(F32)
    lens_col = jnp.transpose(jnp.broadcast_to(lens_row, (rows, rows)))
    lens_b[...] = lens_col
    lane = lax.broadcasted_iota(jnp.int32, (rows, 2 * dim), 1)
    low = lane < dim
    first = (lane & (dim - 1)) < dim // 2
    angles = lens_col * freq_ref[...]
    cos_t = jnp.cos(angles)
    sin_t = jnp.where(first, -jnp.sin(angles), jnp.sin(angles))

    def rope(vals):
        partner = jnp.where(first, pltpu.roll(vals, 2 * dim - dim // 2, 1), pltpu.roll(vals, dim // 2, 1))
        return vals * cos_t + partner * sin_t

    w_copies[1].wait()
    w_copies[2].wait()
    kv = lax.dot_general(normed, wkv_v[...], NT, preferred_element_type=F32)
    bkv = jnp.concatenate([bk_ref[...].astype(F32).reshape(1, dim), bv_ref[...].astype(F32).reshape(1, dim)], axis=1)
    kv = kv + bkv
    kv = jnp.where(low, rope(kv), kv).astype(BF16).astype(F32)
    kvt[...] = jnp.transpose(kv).astype(BF16)
    w_copies[0].wait()
    q_all = jnp.dot(normed, wq_v[...], preferred_element_type=F32) + bq_ref[...].astype(F32).reshape(1, -1)
    for half in range(2):
        q_half = rope(q_all[:, half * 2 * dim:(half + 1) * 2 * dim]).astype(BF16).astype(F32)
        swapped = pltpu.roll(q_half, dim, 1)
        qq[2 * half] = jnp.where(low, q_half, swapped)
        qq[2 * half + 1] = jnp.where(low, swapped, q_half)

    def body(step, carry):
        k_copy, v_copy, k_back, v_back = moves(step)
        base = pl.multiple_of(step * span, span)
        row0 = pl.multiple_of(step * (SEQ * SUB), SEQ * SUB)
        count = SEQ * SUB
        pick = (lax.broadcasted_iota(jnp.int32, (rows, count * 128), 0)
                == row0 + (lax.broadcasted_iota(jnp.int32, (rows, count * 128), 1) >> 7))
        fresh = jnp.dot(kvt[...], jnp.where(pick, 1.0, 0.0).astype(BF16), preferred_element_type=F32)
        k_copy.wait()
        v_copy.wait()
        lane_id = lax.broadcasted_iota(jnp.int32, (dim, 128), 1)
        for i in range(count):
            length = lens_s[row0 + i]
            start = pl.multiple_of((length >> 7) << 7, 128)
            hit = lane_id == (length - start)
            tile = fresh[:, i * 128:(i + 1) * 128]
            where_k = (pl.ds(base + i * dim, dim), pl.ds(start, 128))
            kbuf[where_k] = jnp.where(hit, tile[:dim], kbuf[where_k].astype(F32)).astype(BF16)
            vbuf[where_k] = jnp.where(hit, tile[dim:], vbuf[where_k].astype(F32)).astype(BF16)
        k_back.start()
        v_back.start()
        own = (lax.broadcasted_iota(jnp.int32, (SEQ, SEQ * dim), 1) // dim
               == lax.broadcasted_iota(jnp.int32, (SEQ, SEQ * dim), 0))
        slot = lax.broadcasted_iota(jnp.int32, (SEQ, slots), 1).astype(F32)
        scores = []
        for s in range(SUB):
            r0 = pl.multiple_of(row0 + s * SEQ, SEQ)
            q_blk = qq[:, pl.ds(r0, SEQ), :]
            wide = jnp.concatenate([q_blk] * (SEQ * dim // q_blk.shape[2]), axis=2)
            lhs = jnp.where(own[None], wide, 0.0).reshape(4 * SEQ, SEQ * dim).astype(BF16)
            keys = kbuf[pl.ds(base + s * SEQ * dim, SEQ * dim), :]
            scores.append(jnp.dot(lhs, keys, preferred_element_type=F32) * (dim ** -0.5))
        probs = []
        for s in range(SUB):
            r0 = pl.multiple_of(row0 + s * SEQ, SEQ)
            limit = lens_b[pl.ds(r0, SEQ), :][:, :1]
            masked = jnp.where((slot <= limit)[None], scores[s].reshape(4, SEQ, slots), -jnp.inf)
            top = jnp.max(masked, axis=-1, keepdims=True)
            weight = jnp.exp(masked - top)
            total = jnp.sum(weight, axis=-1, keepdims=True)
            probs.append((weight / total).reshape(4 * SEQ, slots).astype(BF16))
        for s in range(SUB):
            r0 = pl.multiple_of(row0 + s * SEQ, SEQ)
            vals = vbuf[pl.ds(base + s * SEQ * dim, SEQ * dim), :]
            out = lax.dot_general(probs[s], vals, NT, preferred_element_type=F32)
            out = jnp.where(own[None], out.reshape(4, SEQ, SEQ * dim), 0.0)
            width = 2 * dim
            fold = out[:, :, :width]
            for j in range(1, SEQ * dim // width):
                fold = fold + out[:, :, j * width:(j + 1) * width]
            fold = fold.reshape(4 * SEQ, width)
            fold = (fold + pltpu.roll(fold, dim, 1)).reshape(4, SEQ, width)
            low8 = lax.broadcasted_iota(jnp.int32, (SEQ, width), 1) < dim
            o_s[pl.ds(r0, SEQ), :width] = jnp.where(low8, fold[0], fold[1])
            o_s[pl.ds(r0, SEQ), width:] = jnp.where(low8, fold[2], fold[3])
        return carry

    lax.fori_loop(0, steps, body, 0)
    wo_copy.wait()
    part[...] = jnp.dot(o_s[...].astype(BF16), wo_v[...], preferred_element_type=F32).astype(BF16)

    def finish(step, carry):
        _, _, k_back, v_back = moves(step)
        k_back.wait()
        v_back.wait()
        return carry

    lax.fori_loop(0, steps, finish, 0)


def attention(x, lens, kc, vc, g, wq, bq, wk, bk, wv, bv, wo):
    rows, width = x.shape
    slots, dim = kc.shape[1], kc.shape[3]
    flat = rows * dim
    kt = jnp.transpose(kc, (0, 2, 3, 1)).reshape(flat, slots)
    vt = jnp.transpose(vc, (0, 2, 3, 1)).reshape(flat, slots)
    inv_freq = np.power(np.float64(THETA), np.arange(dim // 2) * (-2.0 / dim)).astype(np.float32)
    freq = jnp.asarray(np.tile(inv_freq, 4)[None, :])
    steps = rows // (SEQ * SUB)
    vmem = pl.BlockSpec(memory_space=pltpu.VMEM)
    hbm = pl.BlockSpec(memory_space=pl.ANY)
    dma = pltpu.SemaphoreType.DMA
    ko, vo, part = pl.pallas_call(
        attn_kernel,
        out_shape=(jax.ShapeDtypeStruct((flat, slots), BF16), jax.ShapeDtypeStruct((flat, slots), BF16),
                   jax.ShapeDtypeStruct((rows, width), BF16)),
        in_specs=[pl.BlockSpec(memory_space=pltpu.SMEM)] + [vmem] * 7 + [hbm] * 6,
        out_specs=(hbm, hbm, vmem),
        scratch_shapes=[pltpu.VMEM((flat, slots), BF16), pltpu.VMEM((flat, slots), BF16),
                        pltpu.VMEM(wq.shape, BF16), pltpu.VMEM((2 * dim, width), BF16), pltpu.VMEM(wo.shape, BF16),
                        pltpu.VMEM((rows, rows), F32), pltpu.VMEM((4, rows, 2 * dim), F32),
                        pltpu.VMEM((2 * dim, rows), BF16), pltpu.VMEM((rows, 4 * dim), F32),
                        dma((steps,)), dma((steps,)), dma((steps,)), dma((steps,)), dma((4,))],
        compiler_params=pltpu.CompilerParams(vmem_limit_bytes=48 * 1024 * 1024),
        name='attn',
    )(lens, lens, x, g, bq, bk, bv, freq, kt, vt, wq, wk.T, wv.T, wo)
    back = lambda c: jnp.transpose(c.reshape(rows, 1, dim, slots), (0, 3, 1, 2))
    return part, back(ko), back(vo)


CHUNK = 512
SLOTS = 20


def tail_kernel(part_ref, x_ref, tok_ref, gm_ref, gf_ref, wg, wu, wd, wh,
                y_out, logp_out, lse_out,
                wg_v, wu_v, wd_v, head_v, last_v, d2d, xs, xr, m_s, y_s, a_s, h_s, p_s, f_s, st_s, st_r,
                w_sem, h_sem, d_send, d_recv, x_send, x_recv, g_send, g_recv, f_send, f_recv, s_send, s_recv, y_sem):
    me = lax.axis_index('tp')
    n_tp = 2 * xs.shape[1]
    chips = n_tp // 2
    xi, core = me // 2, me % 2
    sibling = {'tp': me + 1 - 2 * core}
    rows, width = part_ref.shape
    half = rows // 2
    piece = half // chips

    w_copies = [pltpu.make_async_copy(wg, wg_v, w_sem.at[0]), pltpu.make_async_copy(wu, wu_v, w_sem.at[1]),
                pltpu.make_async_copy(wd, wd_v, w_sem.at[2])]
    for copy in w_copies:
        copy.start()
    vocab = wh.shape[0]
    full = vocab // CHUNK
    rest = vocab - full * CHUNK

    def head_copy(i):
        slot = lax.rem(i, SLOTS)
        return pltpu.make_async_copy(wh.at[pl.ds(pl.multiple_of(i * CHUNK, CHUNK), CHUNK)], head_v.at[slot], h_sem.at[slot])

    def head_begin(i, carry):
        head_copy(i).start()
        return carry

    lax.fori_loop(0, min(SLOTS, full), head_begin, 0)
    last_copy = pltpu.make_async_copy(wh.at[pl.ds(full * CHUNK, rest)], last_v, w_sem.at[3])
    last_copy.start()

    barrier = pltpu.get_barrier_semaphore()
    for k in range(1, n_tp):
        pl.semaphore_signal(barrier, inc=1, device_id={'tp': lax.rem(me + k, n_tp)}, device_id_type=MESH)
    pl.semaphore_wait(barrier, n_tp - 1)

    def rows_of(side, chip):
        return pl.ds(pl.multiple_of(side * half + chip * piece, piece), piece)

    def exchange(rnd, src, full_ref, finish):
        order = [2, 1, 3]

        def pair_copy(k):
            chip = lax.rem(xi + k, chips)
            return pltpu.make_async_remote_copy(
                src_ref=src.at[rows_of(1 - core, chip)], dst_ref=d2d.at[rnd, k],
                send_sem=d_send.at[rnd, k], recv_sem=d_recv.at[rnd, k], device_id=sibling, device_id_type=MESH)

        def ring_copy(k):
            return pltpu.make_async_remote_copy(
                src_ref=xs.at[rnd, k], dst_ref=xr.at[rnd, k], send_sem=x_send.at[rnd, k], recv_sem=x_recv.at[rnd, k],
                device_id={'tp': lax.rem(xi + k, chips) * 2 + core}, device_id_type=MESH)

        mine = rows_of(core, xi)

        def share_copy(k):
            return pltpu.make_async_remote_copy(
                src_ref=full_ref.at[mine], dst_ref=full_ref.at[mine], send_sem=g_send.at[rnd, k], recv_sem=g_recv.at[rnd, k],
                device_id={'tp': lax.rem(xi + k, chips) * 2 + core}, device_id_type=MESH)

        def forward_copy(k):
            its = rows_of(core, lax.rem(xi + chips - k, chips))
            return pltpu.make_async_remote_copy(
                src_ref=full_ref.at[its], dst_ref=full_ref.at[its], send_sem=f_send.at[rnd, k], recv_sem=f_recv.at[rnd, k],
                device_id=sibling, device_id_type=MESH)

        for k in order + [0]:
            pair_copy(k).start()
        for k in order:
            pair_copy(k).wait_recv()
            chip = lax.rem(xi + k, chips)
            xs[rnd, k] = (src[rows_of(core, chip), :].astype(F32) + d2d[rnd, k].astype(F32)).astype(BF16)
            ring_copy(k).start()
        pair_copy(0).wait_recv()
        total = src[mine, :].astype(F32) + d2d[rnd, 0].astype(F32)
        for k in (1, 3, 2):
            ring_copy(k).wait_recv()
            total = total + xr[rnd, k].astype(F32)
        full_ref[mine, :] = finish(total)
        for k in order:
            share_copy(k).start()
        forward_copy(0).start()
        for k in (1, 3, 2):
            share_copy(k).wait_recv()
            forward_copy(k).start()
        for k in range(chips):
            forward_copy(k).wait_recv()
        for k in range(chips):
            pair_copy(k).wait_send()
            forward_copy(k).wait_send()
            if k:
                ring_copy(k).wait_send()
                share_copy(k).wait_send()

    mine = rows_of(core, xi)

    def finish_attn(total):
        a = (x_ref[mine, :].astype(F32) + total).astype(BF16)
        a_s[...] = a
        return rms(a.astype(F32), gm_ref[...].astype(F32).reshape(1, -1))

    exchange(0, part_ref, m_s, finish_attn)

    w_copies[0].wait()
    w_copies[1].wait()
    ff = wg_v.shape[1]

    def gate_up(j, carry):
        cols = pl.ds(pl.multiple_of(j * 256, 256), 256)
        gate = jnp.dot(m_s[...], wg_v[:, cols], preferred_element_type=F32)
        up = jnp.dot(m_s[...], wu_v[:, cols], preferred_element_type=F32)
        h_s[:, cols] = (gate * jax.nn.sigmoid(gate) * up).astype(BF16)
        return carry

    lax.fori_loop(0, ff // 256, gate_up, 0)
    w_copies[2].wait()

    def down(j, carry):
        cols = pl.ds(pl.multiple_of(j * 512, 512), 512)
        p_s[:, cols] = jnp.dot(h_s[...], wd_v[:, cols], preferred_element_type=F32).astype(BF16)
        return carry

    lax.fori_loop(0, width // 512, down, 0)

    exchange(1, p_s, y_s, lambda total: (a_s[...].astype(F32) + total).astype(BF16))

    y_copy = pltpu.make_async_copy(y_s, y_out, y_sem)
    y_copy.start()
    gain = gf_ref[...].astype(F32).reshape(1, -1)
    f_s[...] = rms(y_s[...].astype(F32), gain)

    local_tok = tok_ref[...].reshape(1, rows) - me * vocab

    def score(weights, first_row, carry):
        top, total, target = carry
        z = lax.dot_general(weights, f_s[...], NT, preferred_element_type=F32)
        z3 = z.reshape(z.shape[0] // 8, 8, rows)
        new_top = jnp.maximum(top, jnp.max(z3, axis=0))
        total = total * jnp.exp(top - new_top) + jnp.sum(jnp.exp(z3 - new_top[None]), axis=0)
        ids = lax.broadcasted_iota(jnp.int32, z.shape, 0)
        hit = ids == (local_tok - first_row)
        target = target + jnp.sum(jnp.where(hit, z, 0.0).reshape(z3.shape), axis=0)
        return new_top, total, target

    zero = jnp.zeros((8, rows), F32)
    last_copy.wait()
    carry = score(last_v[...], full * CHUNK, (jnp.full((8, rows), -1e30, F32), zero, zero))

    def head_step(i, carry):
        head_copy(i).wait()
        slot = lax.rem(i, SLOTS)
        carry = score(head_v[slot], i * CHUNK, carry)

        @pl.when(i + SLOTS < full)
        def _():
            head_copy(i + SLOTS).start()

        return carry

    top8, total8, target8 = lax.fori_loop(0, full, head_step, carry)
    top = jnp.max(top8, axis=0, keepdims=True)
    total = jnp.sum(total8 * jnp.exp(top8 - top), axis=0, keepdims=True)
    target = jnp.sum(target8, axis=0, keepdims=True)
    st_s[...] = jnp.concatenate([top, total, target, jnp.zeros((5, rows), F32)], axis=0)

    def stat_copy(k):
        return pltpu.make_async_remote_copy(
            src_ref=st_s, dst_ref=st_r.at[k], send_sem=s_send.at[k], recv_sem=s_recv.at[k],
            device_id={'tp': lax.rem(me + k, n_tp)}, device_id_type=MESH)

    for k in range(1, n_tp):
        stat_copy(k).start()
    y_copy.wait()
    for k in range(1, n_tp):
        stat_copy(k).wait_recv()
    tops = [top] + [st_r[k, 0:1, :] for k in range(1, n_tp)]
    totals = [total] + [st_r[k, 1:2, :] for k in range(1, n_tp)]
    best = functools.reduce(jnp.maximum, tops)
    mass = sum(s * jnp.exp(t - best) for s, t in zip(totals, tops))
    hit = target + sum(st_r[k, 2:3, :] for k in range(1, n_tp))
    lse = best + jnp.log(mass)
    lse_out[...] = lse.reshape(rows)
    logp_out[...] = (hit - lse).reshape(rows)
    for k in range(1, n_tp):
        stat_copy(k).wait_send()


def tail(part, x, tok, gm, gf, wg, wu, wd, wh, n_tp):
    rows, width = x.shape
    chips = n_tp // 2
    piece = rows // n_tp
    vmem = pl.BlockSpec(memory_space=pltpu.VMEM)
    hbm = pl.BlockSpec(memory_space=pl.ANY)
    dma = pltpu.SemaphoreType.DMA
    rest = wh.shape[0] % CHUNK
    return pl.pallas_call(
        tail_kernel,
        out_shape=(jax.ShapeDtypeStruct((rows, width), BF16), jax.ShapeDtypeStruct((rows,), F32),
                   jax.ShapeDtypeStruct((rows,), F32)),
        in_specs=[vmem] * 5 + [hbm] * 4,
        out_specs=(hbm, vmem, vmem),
        scratch_shapes=[pltpu.VMEM(wg.shape, BF16), pltpu.VMEM(wu.shape, BF16), pltpu.VMEM(wd.shape, BF16),
                        pltpu.VMEM((SLOTS, CHUNK, width), BF16), pltpu.VMEM((rest, width), BF16),
                        pltpu.VMEM((2, chips, piece, width), BF16), pltpu.VMEM((2, chips, piece, width), BF16),
                        pltpu.VMEM((2, chips, piece, width), BF16),
                        pltpu.VMEM((rows, width), BF16), pltpu.VMEM((rows, width), BF16),
                        pltpu.VMEM((piece, width), BF16), pltpu.VMEM((rows, wg.shape[1]), BF16),
                        pltpu.VMEM((rows, width), BF16), pltpu.VMEM((rows, width), BF16),
                        pltpu.VMEM((8, rows), F32), pltpu.VMEM((n_tp, 8, rows), F32),
                        dma((4,)), dma((SLOTS,)),
                        dma((2, chips)), dma((2, chips)), dma((2, chips)), dma((2, chips)),
                        dma((2, chips)), dma((2, chips)), dma((2, chips)), dma((2, chips)),
                        dma((n_tp,)), dma((n_tp,)), dma],
        compiler_params=pltpu.CompilerParams(vmem_limit_bytes=67043328, collective_id=0, has_side_effects=True),
        name='tail',
    )(part, x, tok, gm, gf, wg, wu, wd, wh)


def solution(mesh):
    n_tp = mesh.shape['tp']

    def local_step(tok_hidden, seq_lens, k_cache, v_cache, next_tok, g_attn, w_q, b_q, w_k, b_k, w_v, b_v, w_o, g_mlp,
                   w_gate, w_up, w_down, g_final, w_head):
        part, k_all, v_all = attention(tok_hidden, seq_lens, k_cache, v_cache, g_attn, w_q, b_q, w_k, b_k, w_v, b_v, w_o)
        y_out, tok_logp, norm_lse = tail(part, tok_hidden, next_tok, g_mlp, g_final, w_gate, w_up, w_down, w_head, n_tp)
        return y_out, k_all, v_all, tok_logp, norm_lse

    row_spec = P('dp', None)
    vec_spec = P('dp')
    cache_spec = P('dp', None, 'tp', None)
    col_spec = P(None, 'tp')
    part_spec = P('tp')
    whole_spec = P(None)
    in_specs = (row_spec, vec_spec, cache_spec, cache_spec, vec_spec, whole_spec, col_spec, part_spec, col_spec, part_spec,
                col_spec, part_spec, P('tp', None), whole_spec, col_spec, col_spec, P('tp', None), whole_spec, P('tp', None))
    out_specs = (row_spec, cache_spec, cache_spec, vec_spec, vec_spec)
    return jax.shard_map(local_step, mesh=mesh, in_specs=in_specs, out_specs=out_specs, check_vma=False)
```

time: 219 us -> 93.3 us (0.43)
  the two profiles are of different devices: /device:TPU:112 before, /device:TPU:113 now
where the time goes in v1:
time: 93.3 us; the launch traced here: 92.8 us
  Pallas kernels  77.9 us (83%)
  local copies, waits for them, and re-layouts  14.3 us (15%)
    pallas_call x1, Pallas kernels, tail(): pl.pallas_call(tail_kernel, out_shape=(jax.ShapeDtypeStruct((rows, width)...  64.1 us
    unnamed x27, local copies, waits for them, and re-layouts  14.3 us
    pallas_call x1, Pallas kernels, attention(): pl.pallas_call(attn_kernel, out_shape=(jax.ShapeDtypeStruct((flat, slots)...  13.8 us

profile of v1, /device:TPU:113, one launch (start us, length us, event | category | flops | bytes accessed | tf_op | source)
XLA Modules:
  0.0 92.8 jit_solution(17315866610791812620)
XLA Ops:
  0.6 0.0 copy-start
  0.6 1.0 %copy-done = bf16[128,2048]{1,0:T(8,128)(2,1)S(1)} copy-done((bf16[128,2048]{1,0:T(8,128)(2,1)S(1)}, bf16[128,2048]{1,0:T(8,128)(2,1)}, u32[]{:S(2)}) %copy-start) | copy-done | bytes 524312
  1.7 0.0 copy-start.1
  1.7 1.2 %copy-done.1 = bf16[2048,256]{1,0:T(8,128)(2,1)S(1)} copy-done((bf16[2048,256]{1,0:T(8,128)(2,1)S(1)}, bf16[2048,256]{1,0:T(8,128)(2,1)}, u32[]{:S(2)}) %copy-start.1) | copy-done | bytes 1048600
  2.9 0.0 copy-start.2
  2.9 1.2 %copy-done.2 = bf16[256,2048]{1,0:T(8,128)(2,1)S(1)} copy-done((bf16[256,2048]{1,0:T(8,128)(2,1)S(1)}, bf16[256,2048]{1,0:T(8,128)(2,1)}, u32[]{:S(2)}) %copy-start.2) | copy-done | bytes 1048600
  4.1 0.0 copy-start.4
  4.1 0.9 %copy-done.4 = bf16[2048,64]{0,1:T(8,128)(2,1)S(1)} copy-done((bf16[2048,64]{0,1:T(8,128)(2,1)S(1)}, bf16[2048,64]{0,1:T(8,128)(2,1)}, u32[]{:S(2)}) %copy-start.4) | copy-done | bytes 262168
  5.1 0.0 copy-start.5
  5.1 0.9 %copy-done.5 = bf16[2048,64]{0,1:T(8,128)(2,1)S(1)} copy-done((bf16[2048,64]{0,1:T(8,128)(2,1)S(1)}, bf16[2048,64]{0,1:T(8,128)(2,1)}, u32[]{:S(2)}) %copy-start.5) | copy-done | bytes 262168
  6.0 0.0 copy-start.6
  6.0 0.7 copy-done.6
  6.7 0.0 copy-start.7
  6.7 0.7 copy-done.7
  7.4 0.0 copy-start.8
  7.4 0.7 copy-done.8
  8.0 0.0 copy-start.9
  8.0 0.7 copy-done.9
  8.7 0.0 copy-start.10
  8.7 0.7 copy-done.10
  9.3 0.0 copy-start.11
  9.3 0.7 copy-done.11
  10.0 13.8 %attn.1 = (bf16[8192,512]{1,0:T(8,128)(2,1)}, bf16[8192,512]{1,0:T(8,128)(2,1)}, bf16[128,2048]{1,0:T(8,128)(2,1)S(1)}) custom-call(s32[128]{0:T(128)S(1)} %copy-done.7, s32[128]{0:T(128)S(1)} %copy-done.7, bf16[128,2048]{1,0:T(8,128)(2,1)S(1)} %copy-done, bf16[2048]{0:T(1024)(128)(2,1)S(1)} %copy-done.6, bf16[256]{0:T(256)(128)(2,1)S(1)} %copy-done.8, ...), custom_call_target="tpu_custom_call" | custom-call | tf_op jit(solution)/shard_map/attn/pallas_call | solution.py:171
  23.8 0.0 copy-start.3
  23.8 0.8 copy-done.3
  24.6 64.1 %tail.1 = (bf16[128,2048]{1,0:T(8,128)(2,1)}, f32[128]{0:T(128)}, f32[128]{0:T(128)}) custom-call(bf16[128,2048]{1,0:T(8,128)(2,1)} %copy-done.3, bf16[128,2048]{1,0:T(8,128)(2,1)} %x_ref.3, s32[128]{0:T(128)} %tok_ref.1, bf16[2048]{0:T(1024)(128)(2,1)} %gm_ref.1, bf16[2048]{0:T(1024)(128)(2,1)} %gf_ref.1, bf16[2048,1024]{1,0:T(8,128)(2,1)} %wg.1, ...), custom_call_target="tpu_custom_call" | custom-call | tf_op jit(solution)/shard_map/tail/pallas_call | solution.py:390
  88.7 1.9 %copy.30 = bf16[128,2048]{1,0:T(8,128)(2,1)} copy(bf16[128,2048]{1,0:T(8,128)(2,1)} %get-tuple-element.22) | data formatting | bytes 1048576
  90.6 1.2 %copy.31 = f32[128]{0:T(128)} copy(f32[128]{0:T(128)} %get-tuple-element.25) | data formatting | bytes 1024
  91.8 1.1 %copy.32 = f32[128]{0:T(128)} copy(f32[128]{0:T(128)} %get-tuple-element.26) | data formatting | bytes 1024
Async XLA Ops:
  0.6 1.0 %copy-start = (bf16[128,2048]{1,0:T(8,128)(2,1)S(1)}, bf16[128,2048]{1,0:T(8,128)(2,1)}, u32[]{:S(2)}) copy-start(bf16[128,2048]{1,0:T(8,128)(2,1)} %x_ref.3) | copy-start | bytes 1572868
  1.7 1.2 %copy-start.1 = (bf16[2048,256]{1,0:T(8,128)(2,1)S(1)}, bf16[2048,256]{1,0:T(8,128)(2,1)}, u32[]{:S(2)}) copy-start(bf16[2048,256]{1,0:T(8,128)(2,1)} %wq.1) | copy-start | bytes 3145732
  2.9 1.2 %copy-start.2 = (bf16[256,2048]{1,0:T(8,128)(2,1)S(1)}, bf16[256,2048]{1,0:T(8,128)(2,1)}, u32[]{:S(2)}) copy-start(bf16[256,2048]{1,0:T(8,128)(2,1)} %wo.1) | copy-start | bytes 3145732
  4.1 0.9 %copy-start.4 = (bf16[2048,64]{0,1:T(8,128)(2,1)S(1)}, bf16[2048,64]{0,1:T(8,128)(2,1)}, u32[]{:S(2)}) copy-start(bf16[2048,64]{0,1:T(8,128)(2,1)} %param.28) | copy-start | bytes 786436
  5.1 0.9 %copy-start.5 = (bf16[2048,64]{0,1:T(8,128)(2,1)S(1)}, bf16[2048,64]{0,1:T(8,128)(2,1)}, u32[]{:S(2)}) copy-start(bf16[2048,64]{0,1:T(8,128)(2,1)} %param.30) | copy-start | bytes 786436
  6.0 0.7 copy-start.6
  6.7 0.7 copy-start.7
  7.4 0.7 copy-start.8
  8.0 0.7 copy-start.9
  8.7 0.7 copy-start.10
  9.3 0.7 copy-start.11
  23.8 0.8 copy-start.3

commit v2 on v1

--- a/solution.py
+++ b/solution.py
@@ -1,5 +1,5 @@
 import functools
-import numpy as np
+import math
 import jax
 import jax.numpy as jnp
 from jax import lax
@@ -20,19 +20,25 @@
     return (vals_f32 * inv_rms * gain_f32).astype(BF16)
 
 
+VMEM_ALL = 67043328
 SEQ = 8
 SUB = 2
 
 
-def attn_kernel(lens_s, lens_v, x_ref, g_ref, bq_ref, bk_ref, bv_ref, freq_ref, kc, vc, wq, wk, wv, wo,
+def attn_kernel(lens, x, g, bq, bk, bv, kc, vc, wq, wk, wv, wo,
                 ko, vo, part, kbuf, vbuf, wq_v, wkv_v, wo_v, lens_b, qq, kvt, o_s,
-                k_in, v_in, k_out, v_out, w_sem):
+                part_s, lens_s, lens_v, x_ref, g_ref, bq_ref, bk_ref, bv_ref,
+                k_in, v_in, k_out, v_out, w_sem, i_sem):
     rows = x_ref.shape[0]
     dim = wk.shape[0]
     slots = kbuf.shape[1]
     span = SEQ * SUB * dim
     steps = kbuf.shape[0] // span
 
+    small = [pltpu.make_async_copy(src, dst, i_sem.at[n]) for n, (src, dst) in enumerate(
+        [(x, x_ref), (g, g_ref), (lens, lens_v), (lens, lens_s), (bq, bq_ref), (bk, bk_ref), (bv, bv_ref)])]
+    for copy in small:
+        copy.start()
     w_copies = [pltpu.make_async_copy(wq, wq_v, w_sem.at[0]),
                 pltpu.make_async_copy(wk, wkv_v.at[pl.ds(0, dim)], w_sem.at[1]),
                 pltpu.make_async_copy(wv, wkv_v.at[pl.ds(dim, dim)], w_sem.at[2])]
@@ -56,6 +62,8 @@
     lax.fori_loop(0, steps, begin, 0)
     wo_copy.start()
 
+    for copy in small:
+        copy.wait()
     normed = rms(x_ref[...].astype(F32), g_ref[...].astype(F32).reshape(1, -1))
     lens_row = lens_v[...].reshape(1, rows).astype(F32)
     lens_col = jnp.transpose(jnp.broadcast_to(lens_row, (rows, rows)))
@@ -63,7 +71,8 @@
     lane = lax.broadcasted_iota(jnp.int32, (rows, 2 * dim), 1)
     low = lane < dim
     first = (lane & (dim - 1)) < dim // 2
-    angles = lens_col * freq_ref[...]
+    power = (lane & (dim // 2 - 1)).astype(F32) * (-2.0 / dim)
+    angles = lens_col * jnp.exp(power * math.log(THETA))
     cos_t = jnp.cos(angles)
     sin_t = jnp.where(first, -jnp.sin(angles), jnp.sin(angles))
 
@@ -145,7 +154,9 @@
 
     lax.fori_loop(0, steps, body, 0)
     wo_copy.wait()
-    part[...] = jnp.dot(o_s[...].astype(BF16), wo_v[...], preferred_element_type=F32).astype(BF16)
+    part_s[...] = jnp.dot(o_s[...].astype(BF16), wo_v[...], preferred_element_type=F32).astype(BF16)
+    part_copy = pltpu.make_async_copy(part_s, part, w_sem.at[4])
+    part_copy.start()
 
     def finish(step, carry):
         _, _, k_back, v_back = moves(step)
@@ -154,6 +165,7 @@
         return carry
 
     lax.fori_loop(0, steps, finish, 0)
+    part_copy.wait()
 
 
 def attention(x, lens, kc, vc, g, wq, bq, wk, bk, wv, bv, wo):
@@ -162,74 +174,134 @@
     flat = rows * dim
     kt = jnp.transpose(kc, (0, 2, 3, 1)).reshape(flat, slots)
     vt = jnp.transpose(vc, (0, 2, 3, 1)).reshape(flat, slots)
-    inv_freq = np.power(np.float64(THETA), np.arange(dim // 2) * (-2.0 / dim)).astype(np.float32)
-    freq = jnp.asarray(np.tile(inv_freq, 4)[None, :])
     steps = rows // (SEQ * SUB)
     vmem = pl.BlockSpec(memory_space=pltpu.VMEM)
-    hbm = pl.BlockSpec(memory_space=pl.ANY)
+    hbm = pl.BlockSpec(memory_space=pltpu.HBM)
     dma = pltpu.SemaphoreType.DMA
     ko, vo, part = pl.pallas_call(
         attn_kernel,
         out_shape=(jax.ShapeDtypeStruct((flat, slots), BF16), jax.ShapeDtypeStruct((flat, slots), BF16),
                    jax.ShapeDtypeStruct((rows, width), BF16)),
-        in_specs=[pl.BlockSpec(memory_space=pltpu.SMEM)] + [vmem] * 7 + [hbm] * 6,
-        out_specs=(hbm, hbm, vmem),
+        in_specs=[hbm] * 12,
+        out_specs=(hbm, hbm, hbm),
         scratch_shapes=[pltpu.VMEM((flat, slots), BF16), pltpu.VMEM((flat, slots), BF16),
                         pltpu.VMEM(wq.shape, BF16), pltpu.VMEM((2 * dim, width), BF16), pltpu.VMEM(wo.shape, BF16),
                         pltpu.VMEM((rows, rows), F32), pltpu.VMEM((4, rows, 2 * dim), F32),
                         pltpu.VMEM((2 * dim, rows), BF16), pltpu.VMEM((rows, 4 * dim), F32),
-                        dma((steps,)), dma((steps,)), dma((steps,)), dma((steps,)), dma((4,))],
-        compiler_params=pltpu.CompilerParams(vmem_limit_bytes=48 * 1024 * 1024),
+                        pltpu.VMEM(x.shape, BF16), pltpu.SMEM((rows,), jnp.int32), pltpu.VMEM((rows,), jnp.int32), pltpu.VMEM(x.shape, BF16),
+                        pltpu.VMEM(g.shape, BF16), pltpu.VMEM(bq.shape, BF16), pltpu.VMEM(bk.shape, BF16),
+                        pltpu.VMEM(bv.shape, BF16),
+                        dma((steps,)), dma((steps,)), dma((steps,)), dma((steps,)), dma((5,)), dma((7,))],
+        compiler_params=pltpu.CompilerParams(vmem_limit_bytes=VMEM_ALL),
         name='attn',
-    )(lens, lens, x, g, bq, bk, bv, freq, kt, vt, wq, wk.T, wv.T, wo)
+    )(lens, x, g, bq, bk, bv, kt, vt, wq, wk.T, wv.T, wo)
     back = lambda c: jnp.transpose(c.reshape(rows, 1, dim, slots), (0, 3, 1, 2))
     return part, back(ko), back(vo)
 
 
 CHUNK = 512
-SLOTS = 20
-
-
-def tail_kernel(part_ref, x_ref, tok_ref, gm_ref, gf_ref, wg, wu, wd, wh,
-                y_out, logp_out, lse_out,
-                wg_v, wu_v, wd_v, head_v, last_v, d2d, xs, xr, m_s, y_s, a_s, h_s, p_s, f_s, st_s, st_r,
-                w_sem, h_sem, d_send, d_recv, x_send, x_recv, g_send, g_recv, f_send, f_recv, s_send, s_recv, y_sem):
+SLOTS = 26
+MLP_SLOTS = 6
+EARLY = 14
+BLOCK = 256
+CHEW = ((0, 7, 3), (0, 5, 5))
+LOW = -1e30
+GROUP = 4
+
+
+def tail_kernel(part, x, tok, gm, gf, wg, wu, wd, wh,
+                y_s, stats,
+                buf, last_v, d2d, xs, xr, m_s, a_s, h_s, p_s, f_s, acc, tok_c, st_s, st_r,
+                part_ref, x_v, tok_v, gm_v, gf_v,
+                w_sem, h_sem, d_send, d_recv, x_send, x_recv, g_send, g_recv, f_send, f_recv, s_send, s_recv):
     me = lax.axis_index('tp')
     n_tp = 2 * xs.shape[1]
     chips = n_tp // 2
     xi, core = me // 2, me % 2
     sibling = {'tp': me + 1 - 2 * core}
-    rows, width = part_ref.shape
+    rows, width = part.shape
     half = rows // 2
     piece = half // chips
-
-    w_copies = [pltpu.make_async_copy(wg, wg_v, w_sem.at[0]), pltpu.make_async_copy(wu, wu_v, w_sem.at[1]),
-                pltpu.make_async_copy(wd, wd_v, w_sem.at[2])]
-    for copy in w_copies:
-        copy.start()
+    ff = wg.shape[1]
     vocab = wh.shape[0]
     full = vocab // CHUNK
     rest = vocab - full * CHUNK
 
+    def rows_of(side, chip):
+        return pl.ds(pl.multiple_of(side * half + chip * piece, piece), piece)
+
+    mine = rows_of(core, xi)
+
+    small = [pltpu.make_async_copy(x.at[mine], x_v, w_sem.at[0]), pltpu.make_async_copy(tok, tok_v, w_sem.at[1]),
+             pltpu.make_async_copy(gm, gm_v, w_sem.at[2]), pltpu.make_async_copy(gf, gf_v, w_sem.at[3]),
+             pltpu.make_async_copy(part, part_ref, w_sem.at[15])]
+    last_copy = pltpu.make_async_copy(wh.at[pl.ds(full * CHUNK, rest)], last_v.at[pl.ds(0, rest)], w_sem.at[4])
+    mlp_copies = []
+    for n, w in enumerate((wg, wu)):
+        for kb in range(width // CHUNK):
+            mlp_copies.append(pltpu.make_async_copy(
+                w.at[pl.ds(kb * CHUNK, CHUNK)], buf.at[2 * n + kb // 2, :, pl.ds((kb % 2) * ff, ff)],
+                w_sem.at[5 + 4 * n + kb]))
+    for kb in range(ff // CHUNK):
+        mlp_copies.append(pltpu.make_async_copy(wd.at[pl.ds(kb * CHUNK, CHUNK)], buf.at[4 + kb], w_sem.at[13 + kb]))
+
+    def slot_of(i):
+        return lax.rem(i + MLP_SLOTS, SLOTS)
+
     def head_copy(i):
-        slot = lax.rem(i, SLOTS)
-        return pltpu.make_async_copy(wh.at[pl.ds(pl.multiple_of(i * CHUNK, CHUNK), CHUNK)], head_v.at[slot], h_sem.at[slot])
+        return pltpu.make_async_copy(wh.at[pl.ds(pl.multiple_of(i * CHUNK, CHUNK), CHUNK)], buf.at[slot_of(i)],
+                                     h_sem.at[slot_of(i)])
 
     def head_begin(i, carry):
         head_copy(i).start()
         return carry
 
-    lax.fori_loop(0, min(SLOTS, full), head_begin, 0)
-    last_copy = pltpu.make_async_copy(wh.at[pl.ds(full * CHUNK, rest)], last_v, w_sem.at[3])
+    for copy in small:
+        copy.start()
+    lax.fori_loop(0, EARLY, head_begin, 0)
+    for copy in mlp_copies:
+        copy.start()
+    lax.fori_loop(EARLY, SLOTS - MLP_SLOTS, head_begin, 0)
     last_copy.start()
 
     barrier = pltpu.get_barrier_semaphore()
     for k in range(1, n_tp):
         pl.semaphore_signal(barrier, inc=1, device_id={'tp': lax.rem(me + k, n_tp)}, device_id_type=MESH)
+
+    last_v[pl.ds(rest, last_v.shape[0] - rest), :] = jnp.zeros((last_v.shape[0] - rest, width), BF16)
+    acc[0] = jnp.full((rows, 128), LOW, F32)
+    acc[1] = jnp.zeros((rows, 128), F32)
+    acc[2] = jnp.zeros((rows, 128), F32)
+    for copy in small:
+        copy.wait()
+    tok_row = (tok_v[...].reshape(1, rows) - me * vocab).astype(F32)
+    tok_row = jnp.where((tok_row >= 0) & (tok_row < vocab), tok_row, -float(2 * vocab))
+    tok_c[...] = jnp.transpose(jnp.broadcast_to(tok_row, (rows, rows))).astype(jnp.int32)
+
     pl.semaphore_wait(barrier, n_tp - 1)
 
-    def rows_of(side, chip):
-        return pl.ds(pl.multiple_of(side * half + chip * piece, piece), piece)
+    turned = [0]
+
+    def chew(count):
+        first = turned[0]
+        turned[0] += count
+
+        def one(i, carry):
+            head_copy(i).wait()
+            slot = slot_of(i)
+
+            def strip(c, inner):
+                cols = pl.ds(pl.multiple_of(c * BLOCK, BLOCK), BLOCK)
+                for r in range(CHUNK // BLOCK):
+                    band = pl.ds(r * BLOCK, BLOCK)
+                    buf[slot, band, cols] = jnp.transpose(buf[slot, band, cols])
+                return inner
+
+            lax.fori_loop(0, width // BLOCK, strip, 0)
+            return carry
+
+        if count:
+            lax.fori_loop(first, first + count, one, 0)
 
     def exchange(rnd, src, full_ref, finish):
         order = [2, 1, 3]
@@ -245,8 +317,6 @@
                 src_ref=xs.at[rnd, k], dst_ref=xr.at[rnd, k], send_sem=x_send.at[rnd, k], recv_sem=x_recv.at[rnd, k],
                 device_id={'tp': lax.rem(xi + k, chips) * 2 + core}, device_id_type=MESH)
 
-        mine = rows_of(core, xi)
-
         def share_copy(k):
             return pltpu.make_async_remote_copy(
                 src_ref=full_ref.at[mine], dst_ref=full_ref.at[mine], send_sem=g_send.at[rnd, k], recv_sem=g_recv.at[rnd, k],
@@ -260,12 +330,14 @@
 
         for k in order + [0]:
             pair_copy(k).start()
+        chew(CHEW[rnd][0])
         for k in order:
             pair_copy(k).wait_recv()
             chip = lax.rem(xi + k, chips)
             xs[rnd, k] = (src[rows_of(core, chip), :].astype(F32) + d2d[rnd, k].astype(F32)).astype(BF16)
             ring_copy(k).start()
         pair_copy(0).wait_recv()
+        chew(CHEW[rnd][1])
         total = src[mine, :].astype(F32) + d2d[rnd, 0].astype(F32)
         for k in (1, 3, 2):
             ring_copy(k).wait_recv()
@@ -274,6 +346,7 @@
         for k in order:
             share_copy(k).start()
         forward_copy(0).start()
+        chew(CHEW[rnd][2])
         for k in (1, 3, 2):
             share_copy(k).wait_recv()
             forward_copy(k).start()
@@ -286,75 +359,112 @@
                 ring_copy(k).wait_send()
                 share_copy(k).wait_send()
 
-    mine = rows_of(core, xi)
-
     def finish_attn(total):
-        a = (x_ref[mine, :].astype(F32) + total).astype(BF16)
+        a = (x_v[...].astype(F32) + total).astype(BF16)
         a_s[...] = a
-        return rms(a.astype(F32), gm_ref[...].astype(F32).reshape(1, -1))
+        return rms(a.astype(F32), gm_v[...].astype(F32).reshape(1, -1))
 
     exchange(0, part_ref, m_s, finish_attn)
 
-    w_copies[0].wait()
-    w_copies[1].wait()
-    ff = wg_v.shape[1]
+    for copy in mlp_copies:
+        copy.wait()
 
     def gate_up(j, carry):
-        cols = pl.ds(pl.multiple_of(j * 256, 256), 256)
-        gate = jnp.dot(m_s[...], wg_v[:, cols], preferred_element_type=F32)
-        up = jnp.dot(m_s[...], wu_v[:, cols], preferred_element_type=F32)
-        h_s[:, cols] = (gate * jax.nn.sigmoid(gate) * up).astype(BF16)
+        def product(n):
+            out = None
+            for kb in range(width // CHUNK):
+                cols = pl.ds(pl.multiple_of((kb % 2) * ff + j * BLOCK, BLOCK), BLOCK)
+                term = jnp.dot(m_s[:, kb * CHUNK:(kb + 1) * CHUNK], buf[2 * n + kb // 2, :, cols], preferred_element_type=F32)
+                out = term if out is None else out + term
+            return out
+
+        gate = product(0)
+        up = product(1)
+        h_s[:, pl.ds(pl.multiple_of(j * BLOCK, BLOCK), BLOCK)] = (gate * jax.nn.sigmoid(gate) * up).astype(BF16)
         return carry
 
-    lax.fori_loop(0, ff // 256, gate_up, 0)
-    w_copies[2].wait()
+    lax.fori_loop(0, ff // BLOCK, gate_up, 0)
 
     def down(j, carry):
-        cols = pl.ds(pl.multiple_of(j * 512, 512), 512)
-        p_s[:, cols] = jnp.dot(h_s[...], wd_v[:, cols], preferred_element_type=F32).astype(BF16)
+        cols = pl.ds(pl.multiple_of(j * CHUNK, CHUNK), CHUNK)
+        out = jnp.dot(h_s[:, :CHUNK], buf[4, :, cols], preferred_element_type=F32)
+        out = out + jnp.dot(h_s[:, CHUNK:], buf[5, :, cols], preferred_element_type=F32)
+        p_s[:, cols] = out.astype(BF16)
         return carry
 
-    lax.fori_loop(0, width // 512, down, 0)
+    lax.fori_loop(0, width // CHUNK, down, 0)
+    lax.fori_loop(SLOTS - MLP_SLOTS, SLOTS, head_begin, 0)
 
     exchange(1, p_s, y_s, lambda total: (a_s[...].astype(F32) + total).astype(BF16))
 
-    y_copy = pltpu.make_async_copy(y_s, y_out, y_sem)
-    y_copy.start()
-    gain = gf_ref[...].astype(F32).reshape(1, -1)
-    f_s[...] = rms(y_s[...].astype(F32), gain)
-
-    local_tok = tok_ref[...].reshape(1, rows) - me * vocab
-
-    def score(weights, first_row, carry):
-        top, total, target = carry
-        z = lax.dot_general(weights, f_s[...], NT, preferred_element_type=F32)
-        z3 = z.reshape(z.shape[0] // 8, 8, rows)
-        new_top = jnp.maximum(top, jnp.max(z3, axis=0))
-        total = total * jnp.exp(top - new_top) + jnp.sum(jnp.exp(z3 - new_top[None]), axis=0)
-        ids = lax.broadcasted_iota(jnp.int32, z.shape, 0)
-        hit = ids == (local_tok - first_row)
-        target = target + jnp.sum(jnp.where(hit, z, 0.0).reshape(z3.shape), axis=0)
-        return new_top, total, target
-
-    zero = jnp.zeros((8, rows), F32)
-    last_copy.wait()
-    carry = score(last_v[...], full * CHUNK, (jnp.full((8, rows), -1e30, F32), zero, zero))
-
-    def head_step(i, carry):
-        head_copy(i).wait()
-        slot = lax.rem(i, SLOTS)
-        carry = score(head_v[slot], i * CHUNK, carry)
-
+    f_s[...] = rms(y_s[...].astype(F32), gf_v[...].astype(F32).reshape(1, -1))
+
+    lane = lax.broadcasted_iota(jnp.int32, (rows, 128), 1)
+
+    def fold(scores, first_row):
+        parts = [scores[:, j * 128:(j + 1) * 128] for j in range(scores.shape[1] // 128)]
+        old = acc[0]
+        top = functools.reduce(jnp.maximum, parts, old)
+        total = acc[1] * jnp.exp(old - top)
+        target = acc[2]
+        place = tok_c[...] - first_row
+        for j, part in enumerate(parts):
+            total = total + jnp.exp(part - top)
+            target = target + jnp.where(place == lane + j * 128, part, 0.0)
+        acc[0] = top
+        acc[1] = total
+        acc[2] = target
+
+    def product(i, r, turned_form):
+        band = pl.ds(r * BLOCK, BLOCK)
+        slot = slot_of(i)
+        if not turned_form:
+            return lax.dot_general(f_s[...], buf[slot, band, :], NT, preferred_element_type=F32)
+        out = None
+        for c in range(width // BLOCK):
+            term = jnp.dot(f_s[:, c * BLOCK:(c + 1) * BLOCK], buf[slot, band, c * BLOCK:(c + 1) * BLOCK],
+                           preferred_element_type=F32)
+            out = term if out is None else out + term
+        return out
+
+    def refill(i):
         @pl.when(i + SLOTS < full)
         def _():
             head_copy(i + SLOTS).start()
 
-        return carry
-
-    top8, total8, target8 = lax.fori_loop(0, full, head_step, carry)
-    top = jnp.max(top8, axis=0, keepdims=True)
-    total = jnp.sum(total8 * jnp.exp(top8 - top), axis=0, keepdims=True)
-    target = jnp.sum(target8, axis=0, keepdims=True)
+    def group(first, size, turned_form):
+        def run(n, carry):
+            base = first + n * size
+            if not turned_form:
+                for u in range(size):
+                    head_copy(base + u).wait()
+            for u in range(size):
+                scores = [product(base + u, r, turned_form) for r in range(CHUNK // BLOCK)]
+                fold(jnp.concatenate(scores, axis=1), (base + u) * CHUNK)
+            for u in range(size):
+                refill(base + u)
+            return carry
+
+        return run
+
+    def sweep(first, count, turned_form):
+        size = min(GROUP, count) if turned_form else 1
+        if count:
+            lax.fori_loop(0, count // size, group(first, size, turned_form), 0)
+            if count % size:
+                lax.fori_loop(0, 1, group(first + count // size * size, count % size, turned_form), 0)
+
+    sweep(0, turned[0], True)
+    sweep(turned[0], full - turned[0], False)
+    last_copy.wait()
+    out = lax.dot_general(f_s[...], last_v[...], NT, preferred_element_type=F32)
+    ids = lax.broadcasted_iota(jnp.int32, out.shape, 1)
+    fold(jnp.where(ids < rest, out, LOW), full * CHUNK)
+
+    tops8 = jnp.transpose(acc[0])
+    top = jnp.max(tops8, axis=0, keepdims=True)
+    total = jnp.sum(jnp.transpose(acc[1]) * jnp.exp(tops8 - top), axis=0, keepdims=True)
+    target = jnp.sum(jnp.transpose(acc[2]), axis=0, keepdims=True)
     st_s[...] = jnp.concatenate([top, total, target, jnp.zeros((5, rows), F32)], axis=0)
 
     def stat_copy(k):
@@ -364,7 +474,6 @@
 
     for k in range(1, n_tp):
         stat_copy(k).start()
-    y_copy.wait()
     for k in range(1, n_tp):
         stat_copy(k).wait_recv()
     tops = [top] + [st_r[k, 0:1, :] for k in range(1, n_tp)]
@@ -373,8 +482,7 @@
     mass = sum(s * jnp.exp(t - best) for s, t in zip(totals, tops))
     hit = target + sum(st_r[k, 2:3, :] for k in range(1, n_tp))
     lse = best + jnp.log(mass)
-    lse_out[...] = lse.reshape(rows)
-    logp_out[...] = (hit - lse).reshape(rows)
+    stats[...] = jnp.concatenate([hit - lse, lse, jnp.zeros((6, rows), F32)], axis=0)
     for k in range(1, n_tp):
         stat_copy(k).wait_send()
 
@@ -384,30 +492,56 @@
     chips = n_tp // 2
     piece = rows // n_tp
     vmem = pl.BlockSpec(memory_space=pltpu.VMEM)
-    hbm = pl.BlockSpec(memory_space=pl.ANY)
+    hbm = pl.BlockSpec(memory_space=pltpu.HBM)
     dma = pltpu.SemaphoreType.DMA
     rest = wh.shape[0] % CHUNK
     return pl.pallas_call(
         tail_kernel,
-        out_shape=(jax.ShapeDtypeStruct((rows, width), BF16), jax.ShapeDtypeStruct((rows,), F32),
-                   jax.ShapeDtypeStruct((rows,), F32)),
-        in_specs=[vmem] * 5 + [hbm] * 4,
-        out_specs=(hbm, vmem, vmem),
-        scratch_shapes=[pltpu.VMEM(wg.shape, BF16), pltpu.VMEM(wu.shape, BF16), pltpu.VMEM(wd.shape, BF16),
-                        pltpu.VMEM((SLOTS, CHUNK, width), BF16), pltpu.VMEM((rest, width), BF16),
+        out_shape=(jax.ShapeDtypeStruct((rows, width), BF16), jax.ShapeDtypeStruct((8, rows), F32)),
+        in_specs=[hbm] * 9,
+        out_specs=(vmem, vmem),
+        scratch_shapes=[pltpu.VMEM((SLOTS, CHUNK, width), BF16), pltpu.VMEM((-(-rest // BLOCK) * BLOCK, width), BF16),
                         pltpu.VMEM((2, chips, piece, width), BF16), pltpu.VMEM((2, chips, piece, width), BF16),
                         pltpu.VMEM((2, chips, piece, width), BF16),
+                        pltpu.VMEM((rows, width), BF16), pltpu.VMEM((piece, width), BF16),
+                        pltpu.VMEM((rows, wg.shape[1]), BF16),
                         pltpu.VMEM((rows, width), BF16), pltpu.VMEM((rows, width), BF16),
-                        pltpu.VMEM((piece, width), BF16), pltpu.VMEM((rows, wg.shape[1]), BF16),
-                        pltpu.VMEM((rows, width), BF16), pltpu.VMEM((rows, width), BF16),
+                        pltpu.VMEM((3, rows, 128), F32), pltpu.VMEM((rows, rows), jnp.int32),
                         pltpu.VMEM((8, rows), F32), pltpu.VMEM((n_tp, 8, rows), F32),
-                        dma((4,)), dma((SLOTS,)),
+                        pltpu.VMEM((rows, width), BF16), pltpu.VMEM((piece, width), BF16), pltpu.VMEM((rows,), jnp.int32),
+                        pltpu.VMEM(gm.shape, BF16), pltpu.VMEM(gf.shape, BF16),
+                        dma((16,)), dma((SLOTS,)),
                         dma((2, chips)), dma((2, chips)), dma((2, chips)), dma((2, chips)),
                         dma((2, chips)), dma((2, chips)), dma((2, chips)), dma((2, chips)),
-                        dma((n_tp,)), dma((n_tp,)), dma],
-        compiler_params=pltpu.CompilerParams(vmem_limit_bytes=67043328, collective_id=0, has_side_effects=True),
+                        dma((n_tp,)), dma((n_tp,))],
+        compiler_params=pltpu.CompilerParams(vmem_limit_bytes=VMEM_TAIL, collective_id=0, has_side_effects=True),
         name='tail',
     )(part, x, tok, gm, gf, wg, wu, wd, wh)
+
+
+VMEM_TAIL = VMEM_ALL
+
+
+def give_kernel(y, stats, y_out, logp_out, lse_out, sem):
+    copy = pltpu.make_async_copy(y, y_out, sem)
+    copy.start()
+    logp_out[...] = stats[0:1, :].reshape(stats.shape[1])
+    lse_out[...] = stats[1:2, :].reshape(stats.shape[1])
+    copy.wait()
+
+
+def give(y, stats):
+    rows = y.shape[0]
+    vmem = pl.BlockSpec(memory_space=pltpu.VMEM)
+    return pl.pallas_call(
+        give_kernel,
+        out_shape=(jax.ShapeDtypeStruct(y.shape, BF16), jax.ShapeDtypeStruct((rows,), F32), jax.ShapeDtypeStruct((rows,), F32)),
+        in_specs=[vmem, vmem],
+        out_specs=(pl.BlockSpec(memory_space=pltpu.HBM), vmem, vmem),
+        scratch_shapes=[pltpu.SemaphoreType.DMA],
+        compiler_params=pltpu.CompilerParams(vmem_limit_bytes=VMEM_TAIL),
+        name='give',
+    )(y, stats)
 
 
 def solution(mesh):
@@ -416,7 +550,8 @@
     def local_step(tok_hidden, seq_lens, k_cache, v_cache, next_tok, g_attn, w_q, b_q, w_k, b_k, w_v, b_v, w_o, g_mlp,
                    w_gate, w_up, w_down, g_final, w_head):
         part, k_all, v_all = attention(tok_hidden, seq_lens, k_cache, v_cache, g_attn, w_q, b_q, w_k, b_k, w_v, b_v, w_o)
-        y_out, tok_logp, norm_lse = tail(part, tok_hidden, next_tok, g_mlp, g_final, w_gate, w_up, w_down, w_head, n_tp)
+        y_all, stats = tail(part, tok_hidden, next_tok, g_mlp, g_final, w_gate, w_up, w_down, w_head, n_tp)
+        y_out, tok_logp, norm_lse = give(y_all, stats)
         return y_out, k_all, v_all, tok_logp, norm_lse
 
     row_spec = P('dp', None)

time: 93.3 us -> 79.8 us (0.86)
  local copies, waits for them, and re-layouts: 14.3 us -> 0 us
  Pallas kernels: 77.9 us -> 79.1 us
    unnamed x27 -> x0, local copies, waits for them, and re-layouts: 14.3 us -> none
    pallas_call x1, Pallas kernels: 64.1 us -> 61.7 us  [tail(): pl.pallas_call(tail_kernel, out_shape=(jax.ShapeDtypeStruct((rows, width)...]
    pallas_call x0 -> x1, Pallas kernels: none -> 2.36 us  [give(): pl.pallas_call(give_kernel, out_shape=(jax.ShapeDtypeStruct(y.shape, BF16...]
    pallas_call x1, Pallas kernels: 13.8 us -> 15 us  [attention(): pl.pallas_call(attn_kernel, out_shape=(jax.ShapeDtypeStruct((flat, slots)...]
where the time goes in v2:
time: 79.8 us; the launch traced here: 79.7 us
  Pallas kernels  79.1 us (99%)
    pallas_call x1, Pallas kernels, tail(): pl.pallas_call(tail_kernel, out_shape=(jax.ShapeDtypeStruct((rows, width)...  61.7 us
    pallas_call x1, Pallas kernels, attention(): pl.pallas_call(attn_kernel, out_shape=(jax.ShapeDtypeStruct((flat, slots)...  15 us
    pallas_call x1, Pallas kernels, give(): pl.pallas_call(give_kernel, out_shape=(jax.ShapeDtypeStruct(y.shape, BF16...  2.36 us

profile of v2, /device:TPU:113, one launch (start us, length us, event | category | flops | bytes accessed | tf_op | source)
XLA Modules:
  0.0 79.7 jit_solution(11771892020243440730)
XLA Ops:
  0.6 15.0 %attn.1 = (bf16[8192,512]{1,0:T(8,128)(2,1)}, bf16[8192,512]{1,0:T(8,128)(2,1)}, bf16[128,2048]{1,0:T(8,128)(2,1)}) custom-call(s32[128]{0:T(128)} %lens.1, bf16[128,2048]{1,0:T(8,128)(2,1)} %x.3, bf16[2048]{0:T(1024)(128)(2,1)} %g.1, bf16[256]{0:T(256)(128)(2,1)} %bq.1, bf16[64]{0:T(256)(128)(2,1)} %bk.1, bf16[64]{0:T(256)(128)(2,1)} %bv.1, ...), custom_call_target="tpu_custom_call" | custom-call | tf_op jit(solution)/shard_map/attn/pallas_call | solution.py:181
  15.7 61.7 %tail.1 = (bf16[128,2048]{1,0:T(8,128)(2,1)}, f32[8,128]{1,0:T(8,128)}) custom-call(bf16[128,2048]{1,0:T(8,128)(2,1)} %get-tuple-element.13.part, bf16[128,2048]{1,0:T(8,128)(2,1)} %x.3, s32[128]{0:T(128)} %tok.1, bf16[2048]{0:T(1024)(128)(2,1)} %gm.1, bf16[2048]{0:T(1024)(128)(2,1)} %gf.1, bf16[2048,1024]{1,0:T(8,128)(2,1)} %wg.1, bf16[2048,1024]{1,0:T(8,128)(2,1)} %wu.1, ...), custom_call_target="tpu_custom_call" | custom-call | tf_op jit(solution)/shard_map/tail/pallas_call | solution.py:498
  77.3 2.4 %give.1 = (bf16[128,2048]{1,0:T(8,128)(2,1)}, f32[128]{0:T(128)}, f32[128]{0:T(128)}) custom-call(bf16[128,2048]{1,0:T(8,128)(2,1)} %get-tuple-element.14.y, f32[8,128]{1,0:T(8,128)} %get-tuple-element.15.stats), custom_call_target="tpu_custom_call" | custom-call | tf_op jit(solution)/shard_map/give/pallas_call | solution.py:536

commit v3 on v2

--- a/solution.py
+++ b/solution.py
@@ -202,16 +202,16 @@
 CHUNK = 512
 SLOTS = 26
 MLP_SLOTS = 6
-EARLY = 14
+EARLY = 10
 BLOCK = 256
-CHEW = ((0, 7, 3), (0, 5, 5))
+CHEW = ((0, 5, 5), (0, 5, 5))
 LOW = -1e30
-GROUP = 4
+GROUP = 3
 
 
 def tail_kernel(part, x, tok, gm, gf, wg, wu, wd, wh,
                 y_s, stats,
-                buf, last_v, d2d, xs, xr, m_s, a_s, h_s, p_s, f_s, acc, tok_c, st_s, st_r,
+                buf, last_v, d2d, xs, xr, m_s, a_s, h_s, p_s, f_s, acc, acd, tok_c, tok_r, st_s, st_r,
                 part_ref, x_v, tok_v, gm_v, gf_v,
                 w_sem, h_sem, d_send, d_recv, x_send, x_recv, g_send, g_recv, f_send, f_recv, s_send, s_recv):
     me = lax.axis_index('tp')
@@ -235,7 +235,7 @@
     small = [pltpu.make_async_copy(x.at[mine], x_v, w_sem.at[0]), pltpu.make_async_copy(tok, tok_v, w_sem.at[1]),
              pltpu.make_async_copy(gm, gm_v, w_sem.at[2]), pltpu.make_async_copy(gf, gf_v, w_sem.at[3]),
              pltpu.make_async_copy(part, part_ref, w_sem.at[15])]
-    last_copy = pltpu.make_async_copy(wh.at[pl.ds(full * CHUNK, rest)], last_v.at[pl.ds(0, rest)], w_sem.at[4])
+    last_copy = pltpu.make_async_copy(wh.at[pl.ds(full * CHUNK, rest)], last_v, w_sem.at[4])
     mlp_copies = []
     for n, w in enumerate((wg, wu)):
         for kb in range(width // CHUNK):
@@ -268,7 +268,9 @@
     for k in range(1, n_tp):
         pl.semaphore_signal(barrier, inc=1, device_id={'tp': lax.rem(me + k, n_tp)}, device_id_type=MESH)
 
-    last_v[pl.ds(rest, last_v.shape[0] - rest), :] = jnp.zeros((last_v.shape[0] - rest, width), BF16)
+    acd[0] = jnp.full((8, rows), LOW, F32)
+    acd[1] = jnp.zeros((8, rows), F32)
+    acd[2] = jnp.zeros((8, rows), F32)
     acc[0] = jnp.full((rows, 128), LOW, F32)
     acc[1] = jnp.zeros((rows, 128), F32)
     acc[2] = jnp.zeros((rows, 128), F32)
@@ -276,6 +278,7 @@
         copy.wait()
     tok_row = (tok_v[...].reshape(1, rows) - me * vocab).astype(F32)
     tok_row = jnp.where((tok_row >= 0) & (tok_row < vocab), tok_row, -float(2 * vocab))
+    tok_r[...] = jnp.broadcast_to(tok_row, (8, rows)).astype(jnp.int32)
     tok_c[...] = jnp.transpose(jnp.broadcast_to(tok_row, (rows, rows))).astype(jnp.int32)
 
     pl.semaphore_wait(barrier, n_tp - 1)
@@ -291,13 +294,11 @@
             slot = slot_of(i)
 
             def strip(c, inner):
-                cols = pl.ds(pl.multiple_of(c * BLOCK, BLOCK), BLOCK)
-                for r in range(CHUNK // BLOCK):
-                    band = pl.ds(r * BLOCK, BLOCK)
-                    buf[slot, band, cols] = jnp.transpose(buf[slot, band, cols])
+                cols = pl.ds(pl.multiple_of(c * CHUNK, CHUNK), CHUNK)
+                buf[slot, :, cols] = jnp.transpose(buf[slot, :, cols])
                 return inner
 
-            lax.fori_loop(0, width // BLOCK, strip, 0)
+            lax.fori_loop(0, width // CHUNK, strip, 0)
             return carry
 
         if count:
@@ -401,7 +402,7 @@
 
     lane = lax.broadcasted_iota(jnp.int32, (rows, 128), 1)
 
-    def fold(scores, first_row):
+    def fold_across(scores, first_row):
         parts = [scores[:, j * 128:(j + 1) * 128] for j in range(scores.shape[1] // 128)]
         old = acc[0]
         top = functools.reduce(jnp.maximum, parts, old)
@@ -415,56 +416,66 @@
         acc[1] = total
         acc[2] = target
 
-    def product(i, r, turned_form):
-        band = pl.ds(r * BLOCK, BLOCK)
+    def fold_down(scores, first_row):
+        groups = scores.reshape(scores.shape[0] // 8, 8, rows)
+        old = acd[0]
+        top = jnp.maximum(old, jnp.max(groups, axis=0))
+        acd[1] = acd[1] * jnp.exp(old - top) + jnp.sum(jnp.exp(groups - top[None]), axis=0)
+        ids = lax.broadcasted_iota(jnp.int32, scores.shape, 0)
+        hit = ids == (tok_r[0:1, :] - first_row)
+        acd[2] = acd[2] + jnp.sum(jnp.where(hit, scores, 0.0).reshape(groups.shape), axis=0)
+        acd[0] = top
+
+    def turned_chunk(i):
         slot = slot_of(i)
-        if not turned_form:
-            return lax.dot_general(f_s[...], buf[slot, band, :], NT, preferred_element_type=F32)
-        out = None
-        for c in range(width // BLOCK):
-            term = jnp.dot(f_s[:, c * BLOCK:(c + 1) * BLOCK], buf[slot, band, c * BLOCK:(c + 1) * BLOCK],
-                           preferred_element_type=F32)
-            out = term if out is None else out + term
-        return out
+        scores = []
+        for r in range(CHUNK // BLOCK):
+            out = None
+            for c in range(width // CHUNK):
+                for n in range(CHUNK // BLOCK):
+                    term = jnp.dot(f_s[:, c * CHUNK + n * BLOCK:c * CHUNK + (n + 1) * BLOCK],
+                                   buf[slot, n * BLOCK:(n + 1) * BLOCK, c * CHUNK + r * BLOCK:c * CHUNK + (r + 1) * BLOCK],
+                                   preferred_element_type=F32)
+                    out = term if out is None else out + term
+            scores.append(out)
+        fold_across(jnp.concatenate(scores, axis=1), i * CHUNK)
+
+    def plain_chunk(i):
+        scores = lax.dot_general(buf[slot_of(i)], f_s[...], NT, preferred_element_type=F32)
+        fold_down(scores, i * CHUNK)
 
     def refill(i):
         @pl.when(i + SLOTS < full)
         def _():
             head_copy(i + SLOTS).start()
 
-    def group(first, size, turned_form):
+    def sweep(first, count, size, take, fresh):
         def run(n, carry):
-            base = first + n * size
-            if not turned_form:
-                for u in range(size):
-                    head_copy(base + u).wait()
-            for u in range(size):
-                scores = [product(base + u, r, turned_form) for r in range(CHUNK // BLOCK)]
-                fold(jnp.concatenate(scores, axis=1), (base + u) * CHUNK)
-            for u in range(size):
-                refill(base + u)
+            at = [first + n * size + u for u in range(size)]
+            if fresh:
+                for i in at:
+                    head_copy(i).wait()
+            for i in at:
+                take(i)
+            for i in at:
+                refill(i)
             return carry
 
-        return run
-
-    def sweep(first, count, turned_form):
-        size = min(GROUP, count) if turned_form else 1
-        if count:
-            lax.fori_loop(0, count // size, group(first, size, turned_form), 0)
-            if count % size:
-                lax.fori_loop(0, 1, group(first + count // size * size, count % size, turned_form), 0)
-
-    sweep(0, turned[0], True)
-    sweep(turned[0], full - turned[0], False)
+        if count >= size:
+            lax.fori_loop(0, count // size, run, 0)
+        if count % size:
+            sweep(first + count // size * size, count % size, count % size, take, fresh)
+
+    sweep(0, turned[0], GROUP, turned_chunk, False)
+    sweep(turned[0], full - turned[0], GROUP, plain_chunk, True)
     last_copy.wait()
-    out = lax.dot_general(f_s[...], last_v[...], NT, preferred_element_type=F32)
-    ids = lax.broadcasted_iota(jnp.int32, out.shape, 1)
-    fold(jnp.where(ids < rest, out, LOW), full * CHUNK)
-
-    tops8 = jnp.transpose(acc[0])
-    top = jnp.max(tops8, axis=0, keepdims=True)
-    total = jnp.sum(jnp.transpose(acc[1]) * jnp.exp(tops8 - top), axis=0, keepdims=True)
-    target = jnp.sum(jnp.transpose(acc[2]), axis=0, keepdims=True)
+    fold_down(lax.dot_general(last_v[...], f_s[...], NT, preferred_element_type=F32), full * CHUNK)
+
+    tops = jnp.transpose(acc[0])
+    top = jnp.maximum(jnp.max(tops, axis=0, keepdims=True), jnp.max(acd[0], axis=0, keepdims=True))
+    total = (jnp.sum(jnp.transpose(acc[1]) * jnp.exp(tops - top), axis=0, keepdims=True)
+             + jnp.sum(acd[1] * jnp.exp(acd[0] - top), axis=0, keepdims=True))
+    target = jnp.sum(jnp.transpose(acc[2]), axis=0, keepdims=True) + jnp.sum(acd[2], axis=0, keepdims=True)
     st_s[...] = jnp.concatenate([top, total, target, jnp.zeros((5, rows), F32)], axis=0)
 
     def stat_copy(k):
@@ -500,13 +511,14 @@
         out_shape=(jax.ShapeDtypeStruct((rows, width), BF16), jax.ShapeDtypeStruct((8, rows), F32)),
         in_specs=[hbm] * 9,
         out_specs=(vmem, vmem),
-        scratch_shapes=[pltpu.VMEM((SLOTS, CHUNK, width), BF16), pltpu.VMEM((-(-rest // BLOCK) * BLOCK, width), BF16),
+        scratch_shapes=[pltpu.VMEM((SLOTS, CHUNK, width), BF16), pltpu.VMEM((rest, width), BF16),
                         pltpu.VMEM((2, chips, piece, width), BF16), pltpu.VMEM((2, chips, piece, width), BF16),
                         pltpu.VMEM((2, chips, piece, width), BF16),
                         pltpu.VMEM((rows, width), BF16), pltpu.VMEM((piece, width), BF16),
                         pltpu.VMEM((rows, wg.shape[1]), BF16),
                         pltpu.VMEM((rows, width), BF16), pltpu.VMEM((rows, width), BF16),
-                        pltpu.VMEM((3, rows, 128), F32), pltpu.VMEM((rows, rows), jnp.int32),
+                        pltpu.VMEM((3, rows, 128), F32), pltpu.VMEM((3, 8, rows), F32),
+                        pltpu.VMEM((rows, rows), jnp.int32), pltpu.VMEM((8, rows), jnp.int32),
                         pltpu.VMEM((8, rows), F32), pltpu.VMEM((n_tp, 8, rows), F32),
                         pltpu.VMEM((rows, width), BF16), pltpu.VMEM((piece, width), BF16), pltpu.VMEM((rows,), jnp.int32),
                         pltpu.VMEM(gm.shape, BF16), pltpu.VMEM(gf.shape, BF16),

time: 79.8 us -> 73.7 us (0.924)
  Pallas kernels: 79.1 us -> 73 us
    pallas_call x1, Pallas kernels: 61.7 us -> 55.6 us  [tail(): pl.pallas_call(tail_kernel, out_shape=(jax.ShapeDtypeStruct((rows, width)...]
where the time goes in v3:
time: 73.7 us; the launch traced here: 73.6 us
  Pallas kernels  73 us (99%)
    pallas_call x1, Pallas kernels, tail(): pl.pallas_call(tail_kernel, out_shape=(jax.ShapeDtypeStruct((rows, width)...  55.6 us
    pallas_call x1, Pallas kernels, attention(): pl.pallas_call(attn_kernel, out_shape=(jax.ShapeDtypeStruct((flat, slots)...  15 us
    pallas_call x1, Pallas kernels, give(): pl.pallas_call(give_kernel, out_shape=(jax.ShapeDtypeStruct(y.shape, BF16...  2.36 us

profile of v3, /device:TPU:113, one launch (start us, length us, event | category | flops | bytes accessed | tf_op | source)
XLA Modules:
  0.0 73.6 jit_solution(10952420568735218299)
XLA Ops:
  0.6 15.0 %attn.1 = (bf16[8192,512]{1,0:T(8,128)(2,1)}, bf16[8192,512]{1,0:T(8,128)(2,1)}, bf16[128,2048]{1,0:T(8,128)(2,1)}) custom-call(s32[128]{0:T(128)} %lens.1, bf16[128,2048]{1,0:T(8,128)(2,1)} %x.3, bf16[2048]{0:T(1024)(128)(2,1)} %g.1, bf16[256]{0:T(256)(128)(2,1)} %bq.1, bf16[64]{0:T(256)(128)(2,1)} %bk.1, bf16[64]{0:T(256)(128)(2,1)} %bv.1, ...), custom_call_target="tpu_custom_call" | custom-call | tf_op jit(solution)/shard_map/attn/pallas_call | solution.py:181
  15.7 55.6 %tail.1 = (bf16[128,2048]{1,0:T(8,128)(2,1)}, f32[8,128]{1,0:T(8,128)}) custom-call(bf16[128,2048]{1,0:T(8,128)(2,1)} %get-tuple-element.13.part, bf16[128,2048]{1,0:T(8,128)(2,1)} %x.3, s32[128]{0:T(128)} %tok.1, bf16[2048]{0:T(1024)(128)(2,1)} %gm.1, bf16[2048]{0:T(1024)(128)(2,1)} %gf.1, bf16[2048,1024]{1,0:T(8,128)(2,1)} %wg.1, bf16[2048,1024]{1,0:T(8,128)(2,1)} %wu.1, ...), custom_call_target="tpu_custom_call" | custom-call | tf_op jit(solution)/shard_map/tail/pallas_call | solution.py:509
  71.3 2.4 %give.1 = (bf16[128,2048]{1,0:T(8,128)(2,1)}, f32[128]{0:T(128)}, f32[128]{0:T(128)}) custom-call(bf16[128,2048]{1,0:T(8,128)(2,1)} %get-tuple-element.14.y, f32[8,128]{1,0:T(8,128)} %get-tuple-element.15.stats), custom_call_target="tpu_custom_call" | custom-call | tf_op jit(solution)/shard_map/give/pallas_call | solution.py:548

commit v4 on v3

--- a/solution.py
+++ b/solution.py
@@ -25,9 +25,9 @@
 SUB = 2
 
 
-def attn_kernel(lens, x, g, bq, bk, bv, kc, vc, wq, wk, wv, wo,
-                ko, vo, part, kbuf, vbuf, wq_v, wkv_v, wo_v, lens_b, qq, kvt, o_s,
-                part_s, lens_s, lens_v, x_ref, g_ref, bq_ref, bk_ref, bv_ref,
+def attn_kernel(lens, x, g, bq, bk, bv, kc, vc, wq, wk, wv,
+                ko, vo, heads, kbuf, vbuf, wq_v, wkv_v, lens_b, qq, kvt, o_s,
+                heads_s, lens_s, lens_v, x_ref, g_ref, bq_ref, bk_ref, bv_ref,
                 k_in, v_in, k_out, v_out, w_sem, i_sem):
     rows = x_ref.shape[0]
     dim = wk.shape[0]
@@ -42,7 +42,6 @@
     w_copies = [pltpu.make_async_copy(wq, wq_v, w_sem.at[0]),
                 pltpu.make_async_copy(wk, wkv_v.at[pl.ds(0, dim)], w_sem.at[1]),
                 pltpu.make_async_copy(wv, wkv_v.at[pl.ds(dim, dim)], w_sem.at[2])]
-    wo_copy = pltpu.make_async_copy(wo, wo_v, w_sem.at[3])
     for copy in w_copies:
         copy.start()
 
@@ -60,7 +59,6 @@
         return carry
 
     lax.fori_loop(0, steps, begin, 0)
-    wo_copy.start()
 
     for copy in small:
         copy.wait()
@@ -153,10 +151,9 @@
         return carry
 
     lax.fori_loop(0, steps, body, 0)
-    wo_copy.wait()
-    part_s[...] = jnp.dot(o_s[...].astype(BF16), wo_v[...], preferred_element_type=F32).astype(BF16)
-    part_copy = pltpu.make_async_copy(part_s, part, w_sem.at[4])
-    part_copy.start()
+    heads_s[...] = o_s[...].astype(BF16)
+    heads_copy = pltpu.make_async_copy(heads_s, heads, w_sem.at[3])
+    heads_copy.start()
 
     def finish(step, carry):
         _, _, k_back, v_back = moves(step)
@@ -165,10 +162,10 @@
         return carry
 
     lax.fori_loop(0, steps, finish, 0)
-    part_copy.wait()
-
-
-def attention(x, lens, kc, vc, g, wq, bq, wk, bk, wv, bv, wo):
+    heads_copy.wait()
+
+
+def attention(x, lens, kc, vc, g, wq, bq, wk, bk, wv, bv):
     rows, width = x.shape
     slots, dim = kc.shape[1], kc.shape[3]
     flat = rows * dim
@@ -178,25 +175,25 @@
     vmem = pl.BlockSpec(memory_space=pltpu.VMEM)
     hbm = pl.BlockSpec(memory_space=pltpu.HBM)
     dma = pltpu.SemaphoreType.DMA
-    ko, vo, part = pl.pallas_call(
+    ko, vo, heads = pl.pallas_call(
         attn_kernel,
         out_shape=(jax.ShapeDtypeStruct((flat, slots), BF16), jax.ShapeDtypeStruct((flat, slots), BF16),
-                   jax.ShapeDtypeStruct((rows, width), BF16)),
-        in_specs=[hbm] * 12,
+                   jax.ShapeDtypeStruct((rows, 4 * dim), BF16)),
+        in_specs=[hbm] * 11,
         out_specs=(hbm, hbm, hbm),
         scratch_shapes=[pltpu.VMEM((flat, slots), BF16), pltpu.VMEM((flat, slots), BF16),
-                        pltpu.VMEM(wq.shape, BF16), pltpu.VMEM((2 * dim, width), BF16), pltpu.VMEM(wo.shape, BF16),
+                        pltpu.VMEM(wq.shape, BF16), pltpu.VMEM((2 * dim, width), BF16),
                         pltpu.VMEM((rows, rows), F32), pltpu.VMEM((4, rows, 2 * dim), F32),
                         pltpu.VMEM((2 * dim, rows), BF16), pltpu.VMEM((rows, 4 * dim), F32),
-                        pltpu.VMEM(x.shape, BF16), pltpu.SMEM((rows,), jnp.int32), pltpu.VMEM((rows,), jnp.int32), pltpu.VMEM(x.shape, BF16),
+                        pltpu.VMEM((rows, 4 * dim), BF16), pltpu.SMEM((rows,), jnp.int32), pltpu.VMEM((rows,), jnp.int32), pltpu.VMEM(x.shape, BF16),
                         pltpu.VMEM(g.shape, BF16), pltpu.VMEM(bq.shape, BF16), pltpu.VMEM(bk.shape, BF16),
                         pltpu.VMEM(bv.shape, BF16),
-                        dma((steps,)), dma((steps,)), dma((steps,)), dma((steps,)), dma((5,)), dma((7,))],
+                        dma((steps,)), dma((steps,)), dma((steps,)), dma((steps,)), dma((4,)), dma((7,))],
         compiler_params=pltpu.CompilerParams(vmem_limit_bytes=VMEM_ALL),
         name='attn',
-    )(lens, x, g, bq, bk, bv, kt, vt, wq, wk.T, wv.T, wo)
+    )(lens, x, g, bq, bk, bv, kt, vt, wq, wk.T, wv.T)
     back = lambda c: jnp.transpose(c.reshape(rows, 1, dim, slots), (0, 3, 1, 2))
-    return part, back(ko), back(vo)
+    return heads, back(ko), back(vo)
 
 
 CHUNK = 512
@@ -206,20 +203,20 @@
 BLOCK = 256
 CHEW = ((0, 5, 5), (0, 5, 5))
 LOW = -1e30
-GROUP = 3
-
-
-def tail_kernel(part, x, tok, gm, gf, wg, wu, wd, wh,
-                y_s, stats,
-                buf, last_v, d2d, xs, xr, m_s, a_s, h_s, p_s, f_s, acc, acd, tok_c, tok_r, st_s, st_r,
-                part_ref, x_v, tok_v, gm_v, gf_v,
+GROUP = 4
+
+
+def tail_kernel(heads, x, tok, gm, gf, wo, wg, wu, wd, wh,
+                y_out, stats,
+                buf, y_s, last_v, d2d, xs, xr, m_s, a_s, h_s, p_s, f_s, o_s, acc, acd, tok_c, tok_r, st_s, st_r,
+                heads_v, x_v, tok_v, gm_v, gf_v,
                 w_sem, h_sem, d_send, d_recv, x_send, x_recv, g_send, g_recv, f_send, f_recv, s_send, s_recv):
     me = lax.axis_index('tp')
     n_tp = 2 * xs.shape[1]
     chips = n_tp // 2
     xi, core = me // 2, me % 2
     sibling = {'tp': me + 1 - 2 * core}
-    rows, width = part.shape
+    rows, width = p_s.shape
     half = rows // 2
     piece = half // chips
     ff = wg.shape[1]
@@ -234,7 +231,8 @@
 
     small = [pltpu.make_async_copy(x.at[mine], x_v, w_sem.at[0]), pltpu.make_async_copy(tok, tok_v, w_sem.at[1]),
              pltpu.make_async_copy(gm, gm_v, w_sem.at[2]), pltpu.make_async_copy(gf, gf_v, w_sem.at[3]),
-             pltpu.make_async_copy(part, part_ref, w_sem.at[15])]
+             pltpu.make_async_copy(heads, heads_v, w_sem.at[15]),
+             pltpu.make_async_copy(wo, buf.at[SLOTS - 1, pl.ds(0, wo.shape[0])], w_sem.at[16])]
     last_copy = pltpu.make_async_copy(wh.at[pl.ds(full * CHUNK, rest)], last_v, w_sem.at[4])
     mlp_copies = []
     for n, w in enumerate((wg, wu)):
@@ -261,7 +259,7 @@
     lax.fori_loop(0, EARLY, head_begin, 0)
     for copy in mlp_copies:
         copy.start()
-    lax.fori_loop(EARLY, SLOTS - MLP_SLOTS, head_begin, 0)
+    lax.fori_loop(EARLY, SLOTS - MLP_SLOTS - 1, head_begin, 0)
     last_copy.start()
 
     barrier = pltpu.get_barrier_semaphore()
@@ -281,6 +279,8 @@
     tok_r[...] = jnp.broadcast_to(tok_row, (8, rows)).astype(jnp.int32)
     tok_c[...] = jnp.transpose(jnp.broadcast_to(tok_row, (rows, rows))).astype(jnp.int32)
 
+    o_s[...] = jnp.dot(heads_v[...], buf[SLOTS - 1, :wo.shape[0], :], preferred_element_type=F32).astype(BF16)
+    head_copy(SLOTS - MLP_SLOTS - 1).start()
     pl.semaphore_wait(barrier, n_tp - 1)
 
     turned = [0]
@@ -304,7 +304,7 @@
         if count:
             lax.fori_loop(first, first + count, one, 0)
 
-    def exchange(rnd, src, full_ref, finish):
+    def exchange(rnd, src, full_ref, finish, landed):
         order = [2, 1, 3]
 
         def pair_copy(k):
@@ -351,8 +351,10 @@
         for k in (1, 3, 2):
             share_copy(k).wait_recv()
             forward_copy(k).start()
+        landed(core)
         for k in range(chips):
             forward_copy(k).wait_recv()
+        landed(1 - core)
         for k in range(chips):
             pair_copy(k).wait_send()
             forward_copy(k).wait_send()
@@ -365,40 +367,32 @@
         a_s[...] = a
         return rms(a.astype(F32), gm_v[...].astype(F32).reshape(1, -1))
 
-    exchange(0, part_ref, m_s, finish_attn)
+    exchange(0, o_s, m_s, finish_attn, lambda side: None)
 
     for copy in mlp_copies:
         copy.wait()
 
-    def gate_up(j, carry):
-        def product(n):
-            out = None
-            for kb in range(width // CHUNK):
-                cols = pl.ds(pl.multiple_of((kb % 2) * ff + j * BLOCK, BLOCK), BLOCK)
-                term = jnp.dot(m_s[:, kb * CHUNK:(kb + 1) * CHUNK], buf[2 * n + kb // 2, :, cols], preferred_element_type=F32)
-                out = term if out is None else out + term
-            return out
-
-        gate = product(0)
-        up = product(1)
-        h_s[:, pl.ds(pl.multiple_of(j * BLOCK, BLOCK), BLOCK)] = (gate * jax.nn.sigmoid(gate) * up).astype(BF16)
-        return carry
-
-    lax.fori_loop(0, ff // BLOCK, gate_up, 0)
-
-    def down(j, carry):
-        cols = pl.ds(pl.multiple_of(j * CHUNK, CHUNK), CHUNK)
-        out = jnp.dot(h_s[:, :CHUNK], buf[4, :, cols], preferred_element_type=F32)
-        out = out + jnp.dot(h_s[:, CHUNK:], buf[5, :, cols], preferred_element_type=F32)
-        p_s[:, cols] = out.astype(BF16)
-        return carry
-
-    lax.fori_loop(0, width // CHUNK, down, 0)
+    def widen(n):
+        out = None
+        for kb in range(width // CHUNK):
+            term = jnp.dot(m_s[:, kb * CHUNK:(kb + 1) * CHUNK], buf[2 * n + kb // 2, :, (kb % 2) * ff:(kb % 2 + 1) * ff],
+                           preferred_element_type=F32)
+            out = term if out is None else out + term
+        return out
+
+    gate = widen(0)
+    h_s[...] = (gate * jax.nn.sigmoid(gate) * widen(1)).astype(BF16)
+    p_s[...] = (jnp.dot(h_s[:, :CHUNK], buf[4], preferred_element_type=F32)
+                + jnp.dot(h_s[:, CHUNK:], buf[5], preferred_element_type=F32)).astype(BF16)
     lax.fori_loop(SLOTS - MLP_SLOTS, SLOTS, head_begin, 0)
 
-    exchange(1, p_s, y_s, lambda total: (a_s[...].astype(F32) + total).astype(BF16))
-
-    f_s[...] = rms(y_s[...].astype(F32), gf_v[...].astype(F32).reshape(1, -1))
+    def final_norm(side):
+        band = pl.ds(pl.multiple_of(side * half, half), half)
+        f_s[band, :] = rms(y_s[band, :].astype(F32), gf_v[...].astype(F32).reshape(1, -1))
+
+    exchange(1, p_s, y_s, lambda total: (a_s[...].astype(F32) + total).astype(BF16), final_norm)
+    y_copy = pltpu.make_async_copy(y_s, y_out, w_sem.at[17])
+    y_copy.start()
 
     lane = lax.broadcasted_iota(jnp.int32, (rows, 128), 1)
 
@@ -485,6 +479,7 @@
 
     for k in range(1, n_tp):
         stat_copy(k).start()
+    y_copy.wait()
     for k in range(1, n_tp):
         stat_copy(k).wait_recv()
     tops = [top] + [st_r[k, 0:1, :] for k in range(1, n_tp)]
@@ -498,7 +493,7 @@
         stat_copy(k).wait_send()
 
 
-def tail(part, x, tok, gm, gf, wg, wu, wd, wh, n_tp):
+def tail(heads, x, tok, gm, gf, wo, wg, wu, wd, wh, n_tp):
     rows, width = x.shape
     chips = n_tp // 2
     piece = rows // n_tp
@@ -509,49 +504,64 @@
     return pl.pallas_call(
         tail_kernel,
         out_shape=(jax.ShapeDtypeStruct((rows, width), BF16), jax.ShapeDtypeStruct((8, rows), F32)),
-        in_specs=[hbm] * 9,
-        out_specs=(vmem, vmem),
-        scratch_shapes=[pltpu.VMEM((SLOTS, CHUNK, width), BF16), pltpu.VMEM((rest, width), BF16),
+        in_specs=[hbm] * 10,
+        out_specs=(hbm, vmem),
+        scratch_shapes=[pltpu.VMEM((SLOTS, CHUNK, width), BF16), pltpu.VMEM((rows, width), BF16), pltpu.VMEM((rest, width), BF16),
                         pltpu.VMEM((2, chips, piece, width), BF16), pltpu.VMEM((2, chips, piece, width), BF16),
                         pltpu.VMEM((2, chips, piece, width), BF16),
                         pltpu.VMEM((rows, width), BF16), pltpu.VMEM((piece, width), BF16),
                         pltpu.VMEM((rows, wg.shape[1]), BF16),
                         pltpu.VMEM((rows, width), BF16), pltpu.VMEM((rows, width), BF16),
-                        pltpu.VMEM((3, rows, 128), F32), pltpu.VMEM((3, 8, rows), F32),
+                        pltpu.VMEM((rows, width), BF16), pltpu.VMEM((3, rows, 128), F32), pltpu.VMEM((3, 8, rows), F32),
                         pltpu.VMEM((rows, rows), jnp.int32), pltpu.VMEM((8, rows), jnp.int32),
                         pltpu.VMEM((8, rows), F32), pltpu.VMEM((n_tp, 8, rows), F32),
-                        pltpu.VMEM((rows, width), BF16), pltpu.VMEM((piece, width), BF16), pltpu.VMEM((rows,), jnp.int32),
+                        pltpu.VMEM(heads.shape, BF16), pltpu.VMEM((piece, width), BF16), pltpu.VMEM((rows,), jnp.int32),
                         pltpu.VMEM(gm.shape, BF16), pltpu.VMEM(gf.shape, BF16),
-                        dma((16,)), dma((SLOTS,)),
+                        dma((18,)), dma((SLOTS,)),
                         dma((2, chips)), dma((2, chips)), dma((2, chips)), dma((2, chips)),
                         dma((2, chips)), dma((2, chips)), dma((2, chips)), dma((2, chips)),
                         dma((n_tp,)), dma((n_tp,))],
         compiler_params=pltpu.CompilerParams(vmem_limit_bytes=VMEM_TAIL, collective_id=0, has_side_effects=True),
         name='tail',
-    )(part, x, tok, gm, gf, wg, wu, wd, wh)
+    )(heads, x, tok, gm, gf, wo, wg, wu, wd, wh)
 
 
 VMEM_TAIL = VMEM_ALL
 
 
-def give_kernel(y, stats, y_out, logp_out, lse_out, sem):
-    copy = pltpu.make_async_copy(y, y_out, sem)
-    copy.start()
-    logp_out[...] = stats[0:1, :].reshape(stats.shape[1])
-    lse_out[...] = stats[1:2, :].reshape(stats.shape[1])
-    copy.wait()
+PIECES = 4
+
+
+def give_kernel(y, stats, y_out, logp_out, lse_out, y_v, s_v, in_sem, out_sem, s_sem):
+    band = [pl.ds(n * (y.shape[0] // PIECES), y.shape[0] // PIECES) for n in range(PIECES)]
+    reads = [pltpu.make_async_copy(y.at[b], y_v.at[b], in_sem.at[n]) for n, b in enumerate(band)]
+    writes = [pltpu.make_async_copy(y_v.at[b], y_out.at[b], out_sem.at[n]) for n, b in enumerate(band)]
+    stat_read = pltpu.make_async_copy(stats, s_v, s_sem)
+    stat_read.start()
+    for read in reads:
+        read.start()
+    stat_read.wait()
+    logp_out[...] = s_v[0:1, :].reshape(s_v.shape[1])
+    lse_out[...] = s_v[1:2, :].reshape(s_v.shape[1])
+    for read, write in zip(reads, writes):
+        read.wait()
+        write.start()
+    for write in writes:
+        write.wait()
 
 
 def give(y, stats):
     rows = y.shape[0]
     vmem = pl.BlockSpec(memory_space=pltpu.VMEM)
+    hbm = pl.BlockSpec(memory_space=pltpu.HBM)
+    dma = pltpu.SemaphoreType.DMA
     return pl.pallas_call(
         give_kernel,
         out_shape=(jax.ShapeDtypeStruct(y.shape, BF16), jax.ShapeDtypeStruct((rows,), F32), jax.ShapeDtypeStruct((rows,), F32)),
-        in_specs=[vmem, vmem],
-        out_specs=(pl.BlockSpec(memory_space=pltpu.HBM), vmem, vmem),
-        scratch_shapes=[pltpu.SemaphoreType.DMA],
-        compiler_params=pltpu.CompilerParams(vmem_limit_bytes=VMEM_TAIL),
+        in_specs=[hbm, hbm],
+        out_specs=(hbm, vmem, vmem),
+        scratch_shapes=[pltpu.VMEM(y.shape, BF16), pltpu.VMEM(stats.shape, F32), dma((PIECES,)), dma((PIECES,)), dma],
+        compiler_params=pltpu.CompilerParams(vmem_limit_bytes=VMEM_ALL),
         name='give',
     )(y, stats)
 
@@ -561,8 +571,8 @@
 
     def local_step(tok_hidden, seq_lens, k_cache, v_cache, next_tok, g_attn, w_q, b_q, w_k, b_k, w_v, b_v, w_o, g_mlp,
                    w_gate, w_up, w_down, g_final, w_head):
-        part, k_all, v_all = attention(tok_hidden, seq_lens, k_cache, v_cache, g_attn, w_q, b_q, w_k, b_k, w_v, b_v, w_o)
-        y_all, stats = tail(part, tok_hidden, next_tok, g_mlp, g_final, w_gate, w_up, w_down, w_head, n_tp)
+        heads, k_all, v_all = attention(tok_hidden, seq_lens, k_cache, v_cache, g_attn, w_q, b_q, w_k, b_k, w_v, b_v)
+        y_all, stats = tail(heads, tok_hidden, next_tok, g_mlp, g_final, w_o, w_gate, w_up, w_down, w_head, n_tp)
         y_out, tok_logp, norm_lse = give(y_all, stats)
         return y_out, k_all, v_all, tok_logp, norm_lse
 

time: 73.7 us -> 71.4 us (0.969)
  Pallas kernels: 73 us -> 70.6 us
    pallas_call x1, Pallas kernels: 55.6 us -> 53.7 us  [tail(): pl.pallas_call(tail_kernel, out_shape=(jax.ShapeDtypeStruct((rows, width)...]
where the time goes in v4:
time: 71.4 us; the launch traced here: 71.3 us
  Pallas kernels  70.6 us (99%)
    pallas_call x1, Pallas kernels, tail(): pl.pallas_call(tail_kernel, out_shape=(jax.ShapeDtypeStruct((rows, width)...  53.7 us
    pallas_call x1, Pallas kernels, attention(): pl.pallas_call(attn_kernel, out_shape=(jax.ShapeDtypeStruct((flat, slots)...  14.6 us
    pallas_call x1, Pallas kernels, give(): pl.pallas_call(give_kernel, out_shape=(jax.ShapeDtypeStruct(y.shape, BF16...  2.35 us

profile of v4, /device:TPU:113, one launch (start us, length us, event | category | flops | bytes accessed | tf_op | source)
XLA Modules:
  0.0 71.3 jit_solution(12250167148625207318)
XLA Ops:
  0.6 14.6 %attn.1 = (bf16[8192,512]{1,0:T(8,128)(2,1)}, bf16[8192,512]{1,0:T(8,128)(2,1)}, bf16[128,256]{1,0:T(8,128)(2,1)}) custom-call(s32[128]{0:T(128)} %lens.1, bf16[128,2048]{1,0:T(8,128)(2,1)} %x.3, bf16[2048]{0:T(1024)(128)(2,1)} %g.1, bf16[256]{0:T(256)(128)(2,1)} %bq.1, bf16[64]{0:T(256)(128)(2,1)} %bk.1, bf16[64]{0:T(256)(128)(2,1)} %bv.1, ...), custom_call_target="tpu_custom_call" | custom-call | tf_op jit(solution)/shard_map/attn/pallas_call | solution.py:178
  15.2 53.7 %tail.1 = (bf16[128,2048]{1,0:T(8,128)(2,1)}, f32[8,128]{1,0:T(8,128)}) custom-call(bf16[128,256]{1,0:T(8,128)(2,1)} %get-tuple-element.13.heads, bf16[128,2048]{1,0:T(8,128)(2,1)} %x.3, s32[128]{0:T(128)} %tok.1, bf16[2048]{0:T(1024)(128)(2,1)} %gm.1, bf16[2048]{0:T(1024)(128)(2,1)} %gf.1, bf16[256,2048]{1,0:T(8,128)(2,1)} %wo.1, bf16[2048,1024]{1,0:T(8,128)(2,1)} %wg.1, ...), custom_call_target="tpu_custom_call" | custom-call | tf_op jit(solution)/shard_map/tail/pallas_call | solution.py:504
  68.9 2.3 %give.1 = (bf16[128,2048]{1,0:T(8,128)(2,1)}, f32[128]{0:T(128)}, f32[128]{0:T(128)}) custom-call(bf16[128,2048]{1,0:T(8,128)(2,1)} %get-tuple-element.14.y, f32[8,128]{1,0:T(8,128)} %get-tuple-element.15.stats), custom_call_target="tpu_custom_call" | custom-call | tf_op jit(solution)/shard_map/give/pallas_call | solution.py:558

commit v5 on v4

--- a/solution.py
+++ b/solution.py
@@ -532,35 +532,38 @@
 PIECES = 4
 
 
-def give_kernel(y, stats, y_out, logp_out, lse_out, y_v, s_v, in_sem, out_sem, s_sem):
+def give_kernel(y, stats, y_out, logp_out, lse_out, y_v, s_v, logp_v, lse_v, in_sem, out_sem, s_sem):
     band = [pl.ds(n * (y.shape[0] // PIECES), y.shape[0] // PIECES) for n in range(PIECES)]
     reads = [pltpu.make_async_copy(y.at[b], y_v.at[b], in_sem.at[n]) for n, b in enumerate(band)]
     writes = [pltpu.make_async_copy(y_v.at[b], y_out.at[b], out_sem.at[n]) for n, b in enumerate(band)]
-    stat_read = pltpu.make_async_copy(stats, s_v, s_sem)
+    stat_read = pltpu.make_async_copy(stats, s_v, s_sem.at[0])
+    sent = [pltpu.make_async_copy(logp_v, logp_out, s_sem.at[1]), pltpu.make_async_copy(lse_v, lse_out, s_sem.at[2])]
     stat_read.start()
     for read in reads:
         read.start()
     stat_read.wait()
-    logp_out[...] = s_v[0:1, :].reshape(s_v.shape[1])
-    lse_out[...] = s_v[1:2, :].reshape(s_v.shape[1])
+    logp_v[...] = s_v[0:1, :].reshape(s_v.shape[1])
+    lse_v[...] = s_v[1:2, :].reshape(s_v.shape[1])
+    for copy in sent:
+        copy.start()
     for read, write in zip(reads, writes):
         read.wait()
         write.start()
-    for write in writes:
-        write.wait()
+    for copy in writes + sent:
+        copy.wait()
 
 
 def give(y, stats):
     rows = y.shape[0]
-    vmem = pl.BlockSpec(memory_space=pltpu.VMEM)
     hbm = pl.BlockSpec(memory_space=pltpu.HBM)
     dma = pltpu.SemaphoreType.DMA
     return pl.pallas_call(
         give_kernel,
         out_shape=(jax.ShapeDtypeStruct(y.shape, BF16), jax.ShapeDtypeStruct((rows,), F32), jax.ShapeDtypeStruct((rows,), F32)),
         in_specs=[hbm, hbm],
-        out_specs=(hbm, vmem, vmem),
-        scratch_shapes=[pltpu.VMEM(y.shape, BF16), pltpu.VMEM(stats.shape, F32), dma((PIECES,)), dma((PIECES,)), dma],
+        out_specs=(hbm, hbm, hbm),
+        scratch_shapes=[pltpu.VMEM(y.shape, BF16), pltpu.VMEM(stats.shape, F32), pltpu.VMEM((rows,), F32), pltpu.VMEM((rows,), F32),
+                        dma((PIECES,)), dma((PIECES,)), dma((3,))],
         compiler_params=pltpu.CompilerParams(vmem_limit_bytes=VMEM_ALL),
         name='give',
     )(y, stats)

time: 71.4 us -> 70.9 us (level)
  no operation moved by 1% of the time
where the time goes in v5:
time: 70.9 us; the launch traced here: 70.8 us
  Pallas kernels  70.1 us (99%)
    pallas_call x1, Pallas kernels, tail(): pl.pallas_call(tail_kernel, out_shape=(jax.ShapeDtypeStruct((rows, width)...  53.7 us
    pallas_call x1, Pallas kernels, attention(): pl.pallas_call(attn_kernel, out_shape=(jax.ShapeDtypeStruct((flat, slots)...  14.6 us
    pallas_call x1, Pallas kernels, give(): pl.pallas_call(give_kernel, out_shape=(jax.ShapeDtypeStruct(y.shape, BF16...  1.85 us

profile of v5, /device:TPU:113, one launch (start us, length us, event | category | flops | bytes accessed | tf_op | source)
XLA Modules:
  0.0 70.8 jit_solution(13152796704372750694)
XLA Ops:
  0.6 14.6 %attn.1 = (bf16[8192,512]{1,0:T(8,128)(2,1)}, bf16[8192,512]{1,0:T(8,128)(2,1)}, bf16[128,256]{1,0:T(8,128)(2,1)}) custom-call(s32[128]{0:T(128)} %lens.1, bf16[128,2048]{1,0:T(8,128)(2,1)} %x.3, bf16[2048]{0:T(1024)(128)(2,1)} %g.1, bf16[256]{0:T(256)(128)(2,1)} %bq.1, bf16[64]{0:T(256)(128)(2,1)} %bk.1, bf16[64]{0:T(256)(128)(2,1)} %bv.1, ...), custom_call_target="tpu_custom_call" | custom-call | tf_op jit(solution)/shard_map/attn/pallas_call | solution.py:178
  15.2 53.7 %tail.1 = (bf16[128,2048]{1,0:T(8,128)(2,1)}, f32[8,128]{1,0:T(8,128)}) custom-call(bf16[128,256]{1,0:T(8,128)(2,1)} %get-tuple-element.13.heads, bf16[128,2048]{1,0:T(8,128)(2,1)} %x.3, s32[128]{0:T(128)} %tok.1, bf16[2048]{0:T(1024)(128)(2,1)} %gm.1, bf16[2048]{0:T(1024)(128)(2,1)} %gf.1, bf16[256,2048]{1,0:T(8,128)(2,1)} %wo.1, bf16[2048,1024]{1,0:T(8,128)(2,1)} %wg.1, ...), custom_call_target="tpu_custom_call" | custom-call | tf_op jit(solution)/shard_map/tail/pallas_call | solution.py:504
  68.9 1.9 %give.1 = (bf16[128,2048]{1,0:T(8,128)(2,1)}, f32[128]{0:T(128)}, f32[128]{0:T(128)}) custom-call(bf16[128,2048]{1,0:T(8,128)(2,1)} %get-tuple-element.14.y, f32[8,128]{1,0:T(8,128)} %get-tuple-element.15.stats), custom_call_target="tpu_custom_call" | custom-call | tf_op jit(solution)/shard_map/give/pallas_call | solution.py:560
